TPU v7x, 32 devices: a whole 2x2x4 slice. The times are simulated.
32 devices in a mesh: section: 8 (over y, x, core), tensor: 4 (over z).
Axes of the slice: x: 2, y: 2, z: 4, core: 2. Of those that a mesh axis runs over, the one named last changes fastest.
Arguments:
- section_inputs: bfloat16 [8, 512, 1024], P('section', 'tensor'), may hold values from -6 to 6
- w_in: bfloat16 [8, 2304, 1024], P('section', 'tensor'), may hold values from -0.1875 to 0.1875
- in_bias: bfloat16 [8, 2304], P('section', 'tensor'), may hold values from -3 to 3
- w_out: bfloat16 [8, 2304, 1024], P('section', 'tensor'), may hold values from -0.125 to 0.125
- out_bias: float32 [8, 1024], P('section'), may hold values from -2 to 2
- norm_gain: float32 [8, 1024], P('section'), may hold values from 0.1 to 1.9
- norm_bias: float32 [8, 1024], P('section'), may hold values from -2 to 2
- patches: bfloat16 [8, 512, 1024], P(None, 'tensor'), may hold values from -6 to 6
- plan: int32 [3], replicated, may hold values from 0 to 7, as said below
Outputs:
- received: bfloat16 [8, 4, 512, 1024], P('section', None, 'tensor')
Inputs may be any that keep to these rules, and one draw needn't show every extreme that they name: `plan`: the first min(8, 3) entries are all different.
All inputs are finite; a program needn't handle non-finite values.
Results may differ from a plain program's by a relative error of at most 0.0065.
Values may be sent and summed in bfloat16 or wider, within the bound.
No kernel may reach another device: no remote copies, remote signals or barrier semaphores. Data moves between devices by JAX's collectives and lax.ppermute only.
A program may use at most 64 MiB of HBM per device.

v0:
```python
import functools

import jax
import jax.numpy as jnp
from jax import lax
from jax.experimental import pallas as pl
from jax.experimental.pallas import tpu as pltpu
from jax.sharding import PartitionSpec as P


TICKS = 4


norm_floor = 0.1
gelu_slope = 1.702


class Plan:
    def __init__(self, sections, tensors):
        self.sections = sections
        self.tensors = tensors
        self.half = tensors // 2

    def side(self, section):
        return (section // 2 + section) % 2

    def stage(self, section):
        return self.half - 1 + self.side(section)

    def device(self, section, tensor):
        return section * self.tensors + tensor

    def worker(self, section, core):
        return self.device(section // 2 * 2 + core, self.stage(section))

    def weight_pairs(self, slot):
        return [
            (
                self.device(section, (self.stage(section) + step) % self.tensors),
                self.worker(section, (section + step) % 2),
            )
            for section in range(self.sections)
            for step in (2 * slot, 2 * slot + 1)
            if step > 0
        ]

    def own_pairs(self, back):
        pairs = [
            (self.worker(section, section % 2), self.worker(section, 1 - section % 2))
            for section in range(self.sections)
        ]
        return [(target, source) for source, target in pairs] if back else pairs

    def token_pairs(self, slot, sections):
        return [
            (self.device(section, core * self.half + slot), self.worker(section, core))
            for section in sections
            for core in range(2)
        ]

    def partner_pairs(self):
        return [
            (self.worker(section, core), self.worker(section, 1 - core))
            for section in range(self.sections)
            for core in range(2)
        ]

    def hop_pairs(self):
        return [
            (self.worker(section, core), self.worker((section + 1) % self.sections, core))
            for section in range(self.sections)
            for core in range(2)
        ]

    def crowded(self, section, tensor):
        return section % 2 == 0 and (tensor >= self.half) != self.side(section)

    def home_pairs(self, slot, shift, crowded=None):
        pairs = []
        for section in range(self.sections):
            for core in range(2):
                tensor = core * self.half + slot
                if crowded is None or self.crowded(section, tensor) == crowded:
                    source = self.worker((section - shift) % self.sections, core)
                    pairs.append((source, self.device(section, tensor)))
        return pairs


def send(value, pairs):
    return lax.ppermute(value, ("section", "tensor"), pairs)


def normalize(current, gain_row, shift_row):
    widened = current.astype(jnp.float32)
    average = jnp.mean(widened, axis=-1, keepdims=True)
    centered = widened - average
    variance = jnp.mean(centered * centered, axis=-1, keepdims=True)
    normed = (centered * lax.rsqrt(variance + norm_floor) * gain_row + shift_row).astype(
        jnp.bfloat16
    )
    return (normed, widened)


def activate(preact):
    return preact * jax.nn.sigmoid(gelu_slope * preact)


def apply_block(current, weights, gain_row, shift_row, bias_row):
    normed, widened = normalize(current, gain_row, shift_row)
    total = None
    for rows_in, rows_bias, rows_out in weights:
        preact = lax.dot_general(
            normed, rows_in, (((1,), (1,)), ((), ())), preferred_element_type=jnp.float32
        )
        hidden = activate(preact + rows_bias).astype(jnp.bfloat16)
        part = jnp.dot(hidden, rows_out, preferred_element_type=jnp.float32)
        total = part if total is None else total + part
    return (widened + total + bias_row).astype(jnp.bfloat16)


OWN, FIRST, CROWDED, SLOT = range(4)


def block_kernel(first_row, n_kept, flags, arrived, fresh, rows, bias, rows_in, rows_out, *refs):
    kept, produced, boxes = refs[:n_kept], refs[n_kept], refs[n_kept + 1 :]
    size = arrived.shape[0]
    if first_row is None:
        current = arrived[...]
    else:
        new = fresh[first_row : first_row + size, :]
        current = jnp.where(flags[FIRST] == 1, new, arrived[...])
    normed, widened = normalize(current, rows[0:1, :], rows[1:2, :])
    preact = lax.dot_general(
        normed, rows_in[...], (((1,), (1,)), ((), ())), preferred_element_type=jnp.float32
    )
    hidden = activate(preact + bias[...]).astype(jnp.bfloat16)
    total = jnp.dot(hidden, rows_out[...], preferred_element_type=jnp.float32)
    result = (widened + total + rows[2:3, :]).astype(jnp.bfloat16)
    produced[...] = result
    if boxes:
        products, arrivals = boxes
        earlier = products.shape[0] // size - 1
        for index in range(earlier):
            products[index * size : (index + 1) * size, :] = kept[index][...]
        products[earlier * size :, :] = result
        for index in range(earlier - 1):
            arrivals[index * size : (index + 1) * size, :] = kept[earlier + index][...]
        arrivals[(earlier - 1) * size :, :] = arrived[...]


def run_block(first_row, flags, arrived, fresh, operands, products=None, arrivals=None):
    vector = pl.BlockSpec(memory_space=pltpu.VMEM)
    chunk = lambda count: jax.ShapeDtypeStruct((count * arrived.shape[0],) + arrived.shape[1:], arrived.dtype)
    shapes, kept = [chunk(1)], []
    if products is not None:
        kept = products + arrivals
        shapes += [chunk(len(products) + 1), chunk(len(arrivals) + 1)]
    return pl.pallas_call(
        functools.partial(block_kernel, first_row, len(kept)),
        out_shape=shapes,
        in_specs=[pl.BlockSpec(memory_space=pltpu.SMEM)] + [vector] * (6 + len(kept)),
        out_specs=[vector] * len(shapes),
        compiler_params=pltpu.CompilerParams(vmem_limit_bytes=8 * 2**20),
        name="section_block",
    )(flags, arrived, fresh, *operands, *kept)


def collect_kernel(slots, flags, *refs):
    records = refs[-1]
    parts = [refs[index * slots : (index + 1) * slots] for index in range(4)]
    from_producer, early, late, final = parts
    size = records.shape[1]
    ticks = records.shape[0]

    def mine(part, start):
        value = part[0][start : start + size, :]
        for slot in range(1, slots):
            value = jnp.where(flags[SLOT] == slot, part[slot][start : start + size, :], value)
        return value

    for tick in range(ticks - 1):
        own = mine(late, 0) if tick == ticks - 2 else mine(early, tick * size)
        records[tick] = jnp.where(flags[CROWDED] == 1, mine(from_producer, tick * size), own)
    records[ticks - 1] = mine(final, 0)


def collect(flags, from_producer, early, late, final):
    vector = pl.BlockSpec(memory_space=pltpu.VMEM)
    pieces = from_producer + early + late + final
    return pl.pallas_call(
        functools.partial(collect_kernel, len(final)),
        out_shape=jax.ShapeDtypeStruct((TICKS,) + final[0].shape, final[0].dtype),
        in_specs=[pl.BlockSpec(memory_space=pltpu.SMEM)] + [vector] * len(pieces),
        out_specs=vector,
        compiler_params=pltpu.CompilerParams(vmem_limit_bytes=8 * 2**20),
        name="collect_quarters",
    )(flags, *pieces)


def assemble_kernel(count, flags, *refs):
    own, other, full, done = refs[:count], refs[count : 2 * count], refs[-2], refs[-1]
    size = own[0].shape[0]

    def place(parts):
        copies = [
            pltpu.make_async_copy(part, full.at[pl.ds(step * size, size)], done.at[step])
            for step, part in enumerate(parts)
        ]
        for copy in copies:
            copy.start()
        for copy in copies:
            copy.wait()

    @pl.when(flags[OWN] == 1)
    def _():
        place(own)

    @pl.when(flags[OWN] == 0)
    def _():
        place(other)


def assemble(flags, own, other):
    main = pl.BlockSpec(memory_space=pltpu.MemorySpace.HBM)
    size, width = own[0].shape
    return pl.pallas_call(
        functools.partial(assemble_kernel, len(own)),
        out_shape=jax.ShapeDtypeStruct((size * len(own), width), own[0].dtype),
        in_specs=[pl.BlockSpec(memory_space=pltpu.SMEM)] + [main] * (2 * len(own)),
        out_specs=pl.BlockSpec(memory_space=pltpu.VMEM),
        scratch_shapes=[pltpu.SemaphoreType.DMA((len(own),))],
        compiler_params=pltpu.CompilerParams(vmem_limit_bytes=8 * 2**20),
        name="assemble_shards",
    )(flags, *own, *other)


def collapsed(section_inputs, w_in, in_bias, w_out, out_bias, norm_gain, norm_bias, patches, plan):
    places = Plan(lax.axis_size("section"), lax.axis_size("tensor"))
    tensors, half = places.tensors, places.half
    section_index = lax.axis_index("section")
    tensor_index = lax.axis_index("tensor")
    core = section_index % 2
    line = section_index // 2
    side = (tensor_index >= half).astype(jnp.int32)
    own_core = (line + side) % 2
    is_own = core == own_core
    is_first = (line == 0) & (own_core == 0)
    is_crowded = (core == 0) & (side != line % 2)
    flags = jnp.stack(
        [flag.astype(jnp.int32) for flag in (is_own, is_first, is_crowded, tensor_index % half)]
    )

    slots = range(half)
    chunk = section_inputs.shape[1]
    everyone = range(places.sections)
    partner = places.partner_pairs()

    def spread(value):
        return [send(value, places.weight_pairs(slot)) for slot in slots]

    def shared(held, received):
        given = send(held, places.own_pairs(False))
        returned = send(received[0], places.own_pairs(True))
        own, other = [held, returned], [given, received[0]]
        for slot in range(1, half):
            swapped = send(received[slot], partner)
            own += [received[slot], swapped]
            other += [swapped, received[slot]]
        return assemble(flags, own, other)

    def tokens(value, sections):
        return [send(value, places.token_pairs(slot, sections)) for slot in slots]

    received_in = spread(w_in[0])
    received_out = spread(w_out[0])
    currents = tokens(section_inputs[0], everyone)
    selected = jnp.concatenate(
        [
            lax.dynamic_index_in_dim(patches, plan[tick_index], 0, keepdims=False)
            for tick_index in range(TICKS - 1)
        ],
        axis=0,
    )
    waiting = tokens(selected, [0])

    biases = [in_bias]
    for step in range(1, tensors):
        pairs = [((place + step) % tensors, place) for place in range(tensors)]
        biases.append(lax.ppermute(in_bias, "tensor", pairs))
    bias = jnp.concatenate(biases, axis=1).astype(jnp.float32)
    rows = jnp.concatenate([norm_gain, norm_bias, out_bias], axis=0)
    bias = jnp.where(is_own, bias, send(bias, partner))
    rows = jnp.where(is_own, rows, send(rows, partner))
    full_in = shared(w_in[0], received_in)
    full_out = shared(w_out[0], received_out)
    operands = (rows, bias, full_in, full_out)

    def home(values, shift, crowded):
        return [send(values[slot], places.home_pairs(slot, shift, crowded)) for slot in slots]

    def hop(values):
        return [send(values[slot], places.hop_pairs()) for slot in slots]

    def block(tick_index, slot, *boxes):
        new = waiting if tick_index else currents
        first_row = (tick_index - 1) * chunk if tick_index else None
        return run_block(first_row, flags, currents[slot], new[slot], operands, *boxes)

    products, arrivals = [[] for _ in slots], [[] for _ in slots]
    for tick_index in range(TICKS - 2):
        for slot in slots:
            products[slot] += block(tick_index, slot)
        currents = hop([made[-1] for made in products])
        for slot in slots:
            arrivals[slot].append(currents[slot])

    boxed = [block(TICKS - 2, slot, products[slot], arrivals[slot][:-1]) for slot in slots]
    currents = hop([box[0] for box in boxed])
    from_producer = home([box[1] for box in boxed], 1, True)
    early = home([box[2] for box in boxed], 0, False)
    late = home(currents, 0, False)
    final = home([block(TICKS - 1, slot)[0] for slot in slots], 1, None)
    return collect(flags, from_producer, early, late, final)[None]


def gathered(section_inputs, w_in, in_bias, w_out, out_bias, norm_gain, norm_bias, patches, plan):
    sections = lax.axis_size("section")
    section_index = lax.axis_index("section")
    gather = lambda value: lax.all_gather(value, "tensor", axis=0, tiled=True)
    full_in, full_bias, full_out = gather(w_in[0]), gather(in_bias[0]), gather(w_out[0])
    weights = [(full_in, full_bias.astype(jnp.float32), full_out)]
    current = section_inputs[0]
    records = []
    for tick_index in range(TICKS):
        produced = apply_block(current, weights, norm_gain[0], norm_bias[0], out_bias[0])
        pairs = [(source, (source + 1) % sections) for source in range(sections)]
        arrived = lax.ppermute(produced, "section", pairs)
        records.append(arrived)
        if tick_index + 1 < TICKS:
            selected = lax.dynamic_index_in_dim(patches, plan[tick_index], 0, keepdims=False)
            current = jnp.where(section_index == 0, selected, arrived)
    return jnp.stack(records, axis=0)[None]


def solution(mesh):
    sections, tensors = mesh.shape["section"], mesh.shape["tensor"]
    fits = sections % 2 == 0 and tensors % 2 == 0 and tensors <= sections // 2
    placed = (
        P("section", "tensor", None),
        P("section", "tensor", None),
        P("section", "tensor"),
        P("section", "tensor", None),
        P("section", None),
        P("section", None),
        P("section", None),
        P(None, "tensor", None),
        P(),
    )

    def body(*args):
        return (collapsed if fits else gathered)(*args)

    return jax.shard_map(
        body,
        mesh=mesh,
        in_specs=placed,
        out_specs=P("section", None, "tensor", None),
        check_vma=False,
    )
```

profile of v0, /device:TPU:5, one launch (start us, length us, event | category | flops | bytes accessed | tf_op | source)
XLA Modules:
  0.0 206.4 jit_solution(4807375006663830610)
XLA Ops:
  1.7 4.3 %collective-permute-start.13 = (bf16[576,1024]{1,0:T(8,128)(2,1)}, bf16[576,1024]{1,0:T(8,128)(2,1)S(1)}, u32[]{:S(2)}, u32[]{:S(2)}) collective-permute-start(bf16[576,1024]{1,0:T(8,128)(2,1)} %bitcast.18), channel_id=1, source_target_pairs={{3,1},{0,5},{4,6},{5,2},{8,10},{9,14},{15,13},{12,9},{19,17},{16,2... | collective-permute-start | bytes 3538952 | tf_op jit(solution)/shard_map/ppermute | solution.py:90
  6.7 1.7 collective-permute-start.6
  8.4 3.1 %collective-permute-start.2 = (bf16[1,576]{1,0:T(2,128)(2,1)}, bf16[1,576]{1,0:T(2,128)(2,1)S(1)}, u32[]{:S(2)}, u32[]{:S(2)}) collective-permute-start(bf16[1,576]{1,0:T(2,128)(2,1)} %param.11), channel_id=1, source_target_pairs={{1,0},{2,1},{3,2},{0,3},{5,4},{6,5},{7,6},{4,7},{9,8},{10,9},{11,1... | collective-permute-start | bytes 3464 | tf_op jit(solution)/shard_map/ppermute | solution.py:289
  11.5 19.7 %collective-permute-done.2 = bf16[1,576]{1,0:T(2,128)(2,1)S(1)} collective-permute-done((bf16[1,576]{1,0:T(2,128)(2,1)}, bf16[1,576]{1,0:T(2,128)(2,1)S(1)}, u32[]{:S(2)}, u32[]{:S(2)}) %collective-permute-start.2) | collective-permute-done | bytes 1184 | tf_op jit(solution)/shard_map/ppermute | solution.py:289
  31.2 14.5 %collective-permute-start.3 = (bf16[1,576]{1,0:T(2,128)(2,1)}, bf16[1,576]{1,0:T(2,128)(2,1)S(1)}, u32[]{:S(2)}, u32[]{:S(2)}) collective-permute-start(bf16[1,576]{1,0:T(2,128)(2,1)} %param.11), channel_id=1, source_target_pairs={{2,0},{3,1},{0,2},{1,3},{6,4},{7,5},{4,6},{5,7},{10,8},{11,9},{8,1... | collective-permute-start | bytes 3464 | tf_op jit(solution)/shard_map/ppermute | solution.py:289
  46.9 4.6 %collective-permute-done.4 = bf16[1,576]{1,0:T(2,128)(2,1)S(1)} collective-permute-done((bf16[1,576]{1,0:T(2,128)(2,1)}, bf16[1,576]{1,0:T(2,128)(2,1)S(1)}, u32[]{:S(2)}, u32[]{:S(2)}) %collective-permute-start.4) | collective-permute-done | bytes 1184 | tf_op jit(solution)/shard_map/ppermute | solution.py:289
  55.0 6.8 %collective-permute-start.8 = (bf16[576,1024]{1,0:T(8,128)(2,1)}, bf16[576,1024]{1,0:T(8,128)(2,1)S(1)}, u32[]{:S(2)}, u32[]{:S(2)}) collective-permute-start(bf16[576,1024]{1,0:T(8,128)(2,1)} %bitcast.22), channel_id=1, source_target_pairs={{3,1},{0,5},{4,6},{5,2},{8,10},{9,14},{15,13},{12,9},{19,17},{16,2... | collective-permute-start | bytes 3538952 | tf_op jit(solution)/shard_map/ppermute | solution.py:90
  61.8 1.7 collective-permute-start.10
  63.5 1.7 collective-permute-start.12
  70.1 16.7 %collective-permute-done.8.refs_2_.refs_7_ = bf16[576,1024]{1,0:T(8,128)(2,1)S(1)} collective-permute-done((bf16[576,1024]{1,0:T(8,128)(2,1)}, bf16[576,1024]{1,0:T(8,128)(2,1)S(1)}, u32[]{:S(2)}, u32[]{:S(2)}) %collective-permute-start.8) | collective-permute-done | bytes 1179680 | tf_op jit(solution)/shard_map/ppermute | solution.py:90
  86.8 1.8 collective-permute-start.9
  97.0 6.4 %collective-permute-start = (bf16[128,1024]{1,0:T(8,128)(2,1)S(1)}, bf16[128,1024]{1,0:T(8,128)(2,1)S(1)}, u32[]{:S(2)}, u32[]{:S(2)}) collective-permute-start(bf16[128,1024]{1,0:T(8,128)(2,1)S(1)} %bitcast.26), channel_id=1, source_target_pairs={{0,1},{2,5},{4,2},{6,6},{8,10},{10,14},{12,9},{14,13},{16,17},{18,... | collective-permute-start | bytes 786440 | tf_op jit(solution)/shard_map/ppermute | solution.py:90
  105.7 2.1 %assemble_shards.3.rows_out = bf16[2304,1024]{1,0:T(8,128)(2,1)S(1)} custom-call(s32[4]{0:T(128)S(1)} %pad_add_fusion.flags, bf16[576,1024]{1,0:T(8,128)(2,1)S(1)} %bitcast.20, bf16[576,1024]{1,0:T(8,128)(2,1)} %collective-permute-done.12.refs_1_, bf16[576,1024]{1,0:T(8,128)(2,1)S(1)} %collective-permute-done.13.refs_2_.refs_7_, ...), custom_call_target="tpu_custom_call" | custom-call | tf_op jit(solution)/shard_map/assemble_shards/pallas_call | solution.py:226
  107.9 2.6 %assemble_shards.2.rows_in = bf16[2304,1024]{1,0:T(8,128)(2,1)S(1)} custom-call(s32[4]{0:T(128)S(1)} %pad_add_fusion.flags, bf16[576,1024]{1,0:T(8,128)(2,1)S(1)} %bitcast.24, bf16[576,1024]{1,0:T(8,128)(2,1)} %collective-permute-done.7.refs_1_, bf16[576,1024]{1,0:T(8,128)(2,1)S(1)} %collective-permute-done.8.refs_2_.refs_7_, ...), custom_call_target="tpu_custom_call" | custom-call | tf_op jit(solution)/shard_map/assemble_shards/pallas_call | solution.py:226
  110.5 3.1 %section_block.11.refs_0_ = bf16[128,1024]{1,0:T(8,128)(2,1)S(1)} custom-call(s32[4]{0:T(128)S(1)} %pad_add_fusion.flags, bf16[128,1024]{1,0:T(8,128)(2,1)S(1)} %collective-permute-done.20.arrived.fresh, bf16[128,1024]{1,0:T(8,128)(2,1)S(1)} %collective-permute-done.20.arrived.fresh, f32[3,1024]{1,0:T(4,128)S(1)} %broadcast_select_fusion.1.rows, ...), custom_call_target="tpu_custom_call" | custom-call | tf_op jit(solution)/shard_map/section_block/pallas_call | solution.py:158
  114.2 3.1 %section_block.8.refs_0_ = bf16[128,1024]{1,0:T(8,128)(2,1)S(1)} custom-call(s32[4]{0:T(128)S(1)} %pad_add_fusion.flags, bf16[128,1024]{1,0:T(8,128)(2,1)S(1)} %collective-permute-done.arrived.fresh, bf16[128,1024]{1,0:T(8,128)(2,1)S(1)} %collective-permute-done.arrived.fresh, f32[3,1024]{1,0:T(4,128)S(1)} %broadcast_select_fusion.1.rows, ...), custom_call_target="tpu_custom_call" | custom-call | tf_op jit(solution)/shard_map/section_block/pallas_call | solution.py:158
  118.0 3.1 %section_block.12.refs_1_ = bf16[128,1024]{1,0:T(8,128)(2,1)S(1)} custom-call(s32[4]{0:T(128)S(1)} %pad_add_fusion.flags, bf16[128,1024]{1,0:T(8,128)(2,1)S(1)} %collective-permute-done.21.arrived.refs_2_, bf16[384,1024]{1,0:T(8,128)(2,1)S(1)} %collective-permute-done.22.fresh, f32[3,1024]{1,0:T(4,128)S(1)} %broadcast_select_fusion.1.rows, ...), custom_call_target="tpu_custom_call" | custom-call | tf_op jit(solution)/shard_map/section_block/pallas_call | solution.py:158
  121.8 3.1 %section_block.9.refs_1_ = bf16[128,1024]{1,0:T(8,128)(2,1)S(1)} custom-call(s32[4]{0:T(128)S(1)} %pad_add_fusion.flags, bf16[128,1024]{1,0:T(8,128)(2,1)S(1)} %collective-permute-done.16.arrived.refs_2_, bf16[384,1024]{1,0:T(8,128)(2,1)S(1)} %collective-permute-done.17.fresh, f32[3,1024]{1,0:T(4,128)S(1)} %broadcast_select_fusion.1.rows, ...), custom_call_target="tpu_custom_call" | custom-call | tf_op jit(solution)/shard_map/section_block/pallas_call | solution.py:158
  125.7 3.0 %section_block.13 = (bf16[128,1024]{1,0:T(8,128)(2,1)S(1)}, bf16[384,1024]{1,0:T(8,128)(2,1)S(1)}, bf16[256,1024]{1,0:T(8,128)(2,1)S(1)}) custom-call(s32[4]{0:T(128)S(1)} %pad_add_fusion.flags, bf16[128,1024]{1,0:T(8,128)(2,1)S(1)} %collective-permute-done.23.arrived, bf16[384,1024]{1,0:T(8,128)(2,1)S(1)} %collective-permute-done.22.fresh, ...), custom_call_target="tpu_custom_call" | custom-call | tf_op jit(solution)/shard_map/section_block/pallas_call | solution.py:158
  129.4 3.1 %section_block.10 = (bf16[128,1024]{1,0:T(8,128)(2,1)S(1)}, bf16[384,1024]{1,0:T(8,128)(2,1)S(1)}, bf16[256,1024]{1,0:T(8,128)(2,1)S(1)}) custom-call(s32[4]{0:T(128)S(1)} %pad_add_fusion.flags, bf16[128,1024]{1,0:T(8,128)(2,1)S(1)} %collective-permute-done.18.arrived, bf16[384,1024]{1,0:T(8,128)(2,1)S(1)} %collective-permute-done.17.fresh, ...), custom_call_target="tpu_custom_call" | custom-call | tf_op jit(solution)/shard_map/section_block/pallas_call | solution.py:158
  133.2 3.1 %section_block.15 = bf16[128,1024]{1,0:T(8,128)(2,1)S(1)} custom-call(s32[4]{0:T(128)S(1)} %pad_add_fusion.flags, bf16[128,1024]{1,0:T(8,128)(2,1)S(1)} %collective-permute-done.29.arrived, bf16[384,1024]{1,0:T(8,128)(2,1)S(1)} %collective-permute-done.22.fresh, f32[3,1024]{1,0:T(4,128)S(1)} %broadcast_select_fusion.1.rows, ...), custom_call_target="tpu_custom_call" | custom-call | tf_op jit(solution)/shard_map/section_block/pallas_call | solution.py:158
  137.0 3.1 %section_block.14 = bf16[128,1024]{1,0:T(8,128)(2,1)S(1)} custom-call(s32[4]{0:T(128)S(1)} %pad_add_fusion.flags, bf16[128,1024]{1,0:T(8,128)(2,1)S(1)} %collective-permute-done.27.arrived, bf16[384,1024]{1,0:T(8,128)(2,1)S(1)} %collective-permute-done.17.fresh, f32[3,1024]{1,0:T(4,128)S(1)} %broadcast_select_fusion.1.rows, ...), custom_call_target="tpu_custom_call" | custom-call | tf_op jit(solution)/shard_map/section_block/pallas_call | solution.py:158
  144.2 22.3 %collective-permute-done.31.refs_6_ = bf16[128,1024]{1,0:T(8,128)(2,1)S(1)} collective-permute-done((bf16[128,1024]{1,0:T(8,128)(2,1)S(1)}, bf16[128,1024]{1,0:T(8,128)(2,1)S(1)}, u32[]{:S(2)}, u32[]{:S(2)}) %collective-permute-start.31) | collective-permute-done | bytes 262176 | tf_op jit(solution)/shard_map/ppermute | solution.py:90
  169.1 35.6 %collective-permute-done.28.refs_4_ = bf16[128,1024]{1,0:T(8,128)(2,1)S(1)} collective-permute-done((bf16[128,1024]{1,0:T(8,128)(2,1)S(1)}, bf16[128,1024]{1,0:T(8,128)(2,1)S(1)}, u32[]{:S(2)}, u32[]{:S(2)}) %collective-permute-start.28) | collective-permute-done | bytes 262176 | tf_op jit(solution)/shard_map/ppermute | solution.py:90
  (82 shorter events, 30.3 us)
Async XLA Ops:
  0.0 61.8 %collective-permute-start.11 = (bf16[576,1024]{1,0:T(8,128)(2,1)}, bf16[576,1024]{1,0:T(8,128)(2,1)}, u32[]{:S(2)}, u32[]{:S(2)}) collective-permute-start(bf16[576,1024]{1,0:T(8,128)(2,1)} %bitcast.17), channel_id=1, source_target_pairs={{2,5},{7,2},{11,14},{14,9},{18,21},{23,18},{27,30},{30,25}} | collective-permute-start | bytes 3538952 | tf_op jit(solution)/shard_map/ppermute | solution.py:90
  1.7 61.8 %collective-permute-start.13 = (bf16[576,1024]{1,0:T(8,128)(2,1)}, bf16[576,1024]{1,0:T(8,128)(2,1)S(1)}, u32[]{:S(2)}, u32[]{:S(2)}) collective-permute-start(bf16[576,1024]{1,0:T(8,128)(2,1)} %bitcast.18), channel_id=1, source_target_pairs={{3,1},{0,5},{4,6},{5,2},{8,10},{9,14},{15,13},{12,9},{19,17},{16,2... | collective-permute-start | bytes 3538952 | tf_op jit(solution)/shard_map/ppermute | solution.py:90
  6.0 59.3 %collective-permute-start.15 = (bf16[576,1024]{1,0:T(8,128)(2,1)}, bf16[576,1024]{1,0:T(8,128)(2,1)S(1)}, u32[]{:S(2)}, u32[]{:S(2)}) collective-permute-start(bf16[576,1024]{1,0:T(8,128)(2,1)} %bitcast.19), channel_id=1, source_target_pairs={{1,5},{6,2},{10,14},{13,9},{17,21},{22,18},{26,30},{29,25}} | collective-permute-start | bytes 3538952 | tf_op jit(solution)/shard_map/ppermute | solution.py:90
  6.7 60.3 %collective-permute-start.6 = (bf16[576,1024]{1,0:T(8,128)(2,1)}, bf16[576,1024]{1,0:T(8,128)(2,1)}, u32[]{:S(2)}, u32[]{:S(2)}) collective-permute-start(bf16[576,1024]{1,0:T(8,128)(2,1)} %bitcast.21), channel_id=1, source_target_pairs={{2,5},{7,2},{11,14},{14,9},{18,21},{23,18},{27,30},{30,25}} | collective-permute-start | bytes 3538952 | tf_op jit(solution)/shard_map/ppermute | solution.py:90
  8.4 22.8 %collective-permute-start.2 = (bf16[1,576]{1,0:T(2,128)(2,1)}, bf16[1,576]{1,0:T(2,128)(2,1)S(1)}, u32[]{:S(2)}, u32[]{:S(2)}) collective-permute-start(bf16[1,576]{1,0:T(2,128)(2,1)} %param.11), channel_id=1, source_target_pairs={{1,0},{2,1},{3,2},{0,3},{5,4},{6,5},{7,6},{4,7},{9,8},{10,9},{11,1... | collective-permute-start | bytes 3464 | tf_op jit(solution)/shard_map/ppermute | solution.py:289
  31.2 15.7 %collective-permute-start.3 = (bf16[1,576]{1,0:T(2,128)(2,1)}, bf16[1,576]{1,0:T(2,128)(2,1)S(1)}, u32[]{:S(2)}, u32[]{:S(2)}) collective-permute-start(bf16[1,576]{1,0:T(2,128)(2,1)} %param.11), channel_id=1, source_target_pairs={{2,0},{3,1},{0,2},{1,3},{6,4},{7,5},{4,6},{5,7},{10,8},{11,9},{8,1... | collective-permute-start | bytes 3464 | tf_op jit(solution)/shard_map/ppermute | solution.py:289
  55.0 31.8 %collective-permute-start.8 = (bf16[576,1024]{1,0:T(8,128)(2,1)}, bf16[576,1024]{1,0:T(8,128)(2,1)S(1)}, u32[]{:S(2)}, u32[]{:S(2)}) collective-permute-start(bf16[576,1024]{1,0:T(8,128)(2,1)} %bitcast.22), channel_id=1, source_target_pairs={{3,1},{0,5},{4,6},{5,2},{8,10},{9,14},{15,13},{12,9},{19,17},{16,2... | collective-permute-start | bytes 3538952 | tf_op jit(solution)/shard_map/ppermute | solution.py:90
  61.8 33.7 %collective-permute-start.10 = (bf16[576,1024]{1,0:T(8,128)(2,1)}, bf16[576,1024]{1,0:T(8,128)(2,1)}, u32[]{:S(2)}, u32[]{:S(2)}) collective-permute-start(bf16[576,1024]{1,0:T(8,128)(2,1)} %bitcast.23), channel_id=1, source_target_pairs={{1,5},{6,2},{10,14},{13,9},{17,21},{22,18},{26,30},{29,25}} | collective-permute-start | bytes 3538952 | tf_op jit(solution)/shard_map/ppermute | solution.py:90
  63.5 33.5 %collective-permute-start.12 = (bf16[576,1024]{1,0:T(8,128)(2,1)}, bf16[576,1024]{1,0:T(8,128)(2,1)}, u32[]{:S(2)}, u32[]{:S(2)}) collective-permute-start(bf16[576,1024]{1,0:T(8,128)(2,1)} %collective-permute-done.11.refs_5_), channel_id=1, source_target_pairs={{5,1},{2,6},{14,10},{9,13},{21,17},{18,22},{30,26},{25,29}} | collective-permute-start | bytes 3538952 | tf_op jit(solution)/shard_map/ppermute | solution.py:90
  66.3 37.2 %collective-permute-start.14 = (bf16[576,1024]{1,0:T(8,128)(2,1)S(1)}, bf16[576,1024]{1,0:T(8,128)(2,1)S(1)}, u32[]{:S(2)}, u32[]{:S(2)}) collective-permute-start(bf16[576,1024]{1,0:T(8,128)(2,1)S(1)} %collective-permute-done.13.refs_2_.refs_7_), channel_id=1, source_target_pairs={{1,5},{5,1},{2,6},{6,2},{10,14},{14,10},{9,13},{13,9},{17,21},{21,... | collective-permute-start | bytes 3538952 | tf_op jit(solution)/shard_map/ppermute | solution.py:90
  67.0 37.2 %collective-permute-start.7 = (bf16[576,1024]{1,0:T(8,128)(2,1)}, bf16[576,1024]{1,0:T(8,128)(2,1)}, u32[]{:S(2)}, u32[]{:S(2)}) collective-permute-start(bf16[576,1024]{1,0:T(8,128)(2,1)} %collective-permute-done.6.refs_5_), channel_id=1, source_target_pairs={{5,1},{2,6},{14,10},{9,13},{21,17},{18,22},{30,26},{25,29}} | collective-permute-start | bytes 3538952 | tf_op jit(solution)/shard_map/ppermute | solution.py:90
  86.8 21.1 %collective-permute-start.9 = (bf16[576,1024]{1,0:T(8,128)(2,1)S(1)}, bf16[576,1024]{1,0:T(8,128)(2,1)}, u32[]{:S(2)}, u32[]{:S(2)}) collective-permute-start(bf16[576,1024]{1,0:T(8,128)(2,1)S(1)} %collective-permute-done.8.refs_2_.refs_7_), channel_id=1, source_target_pairs={{1,5},{5,1},{2,6},{6,2},{10,14},{14,10},{9,13},{13,9},{17,21},{21,... | collective-permute-start | bytes 3538952 | tf_op jit(solution)/shard_map/ppermute | solution.py:90
  96.4 14.1 %collective-permute-start.20 = (bf16[128,1024]{1,0:T(8,128)(2,1)S(1)}, bf16[128,1024]{1,0:T(8,128)(2,1)S(1)}, u32[]{:S(2)}, u32[]{:S(2)}) collective-permute-start(bf16[128,1024]{1,0:T(8,128)(2,1)S(1)} %bitcast.25), channel_id=1, source_target_pairs={{1,1},{3,5},{5,2},{7,6},{9,10},{11,14},{13,9},{15,13},{17,17},{19,... | collective-permute-start | bytes 786440 | tf_op jit(solution)/shard_map/ppermute | solution.py:90
  97.0 17.2 %collective-permute-start = (bf16[128,1024]{1,0:T(8,128)(2,1)S(1)}, bf16[128,1024]{1,0:T(8,128)(2,1)S(1)}, u32[]{:S(2)}, u32[]{:S(2)}) collective-permute-start(bf16[128,1024]{1,0:T(8,128)(2,1)S(1)} %bitcast.26), channel_id=1, source_target_pairs={{0,1},{2,5},{4,2},{6,6},{8,10},{10,14},{12,9},{14,13},{16,17},{18,... | collective-permute-start | bytes 786440 | tf_op jit(solution)/shard_map/ppermute | solution.py:90
  103.4 14.5 %collective-permute-start.22 = (bf16[384,1024]{1,0:T(8,128)(2,1)S(1)}, bf16[384,1024]{1,0:T(8,128)(2,1)S(1)}, u32[]{:S(2)}, u32[]{:S(2)}) collective-permute-start(bf16[384,1024]{1,0:T(8,128)(2,1)S(1)} %pad_maximum_fusion), channel_id=1, source_target_pairs={{1,1},{3,5}} | collective-permute-start | bytes 2359304 | tf_op jit(solution)/shard_map/ppermute | solution.py:90
  104.2 17.6 %collective-permute-start.17 = (bf16[384,1024]{1,0:T(8,128)(2,1)S(1)}, bf16[384,1024]{1,0:T(8,128)(2,1)S(1)}, u32[]{:S(2)}, u32[]{:S(2)}) collective-permute-start(bf16[384,1024]{1,0:T(8,128)(2,1)S(1)} %pad_maximum_fusion), channel_id=1, source_target_pairs={{0,1},{2,5}} | collective-permute-start | bytes 2359304 | tf_op jit(solution)/shard_map/ppermute | solution.py:90
  136.3 7.2 %collective-permute-start.32 = (bf16[128,1024]{1,0:T(8,128)(2,1)S(1)}, bf16[128,1024]{1,0:T(8,128)(2,1)S(1)}, u32[]{:S(2)}, u32[]{:S(2)}) collective-permute-start(bf16[128,1024]{1,0:T(8,128)(2,1)S(1)} %section_block.15), channel_id=1, source_target_pairs={{25,1},{29,3},{1,5},{5,7},{2,9},{6,11},{10,13},{14,15},{9,17},{13,... | collective-permute-start | bytes 786440 | tf_op jit(solution)/shard_map/ppermute | solution.py:90
  140.0 26.4 %collective-permute-start.31 = (bf16[128,1024]{1,0:T(8,128)(2,1)S(1)}, bf16[128,1024]{1,0:T(8,128)(2,1)S(1)}, u32[]{:S(2)}, u32[]{:S(2)}) collective-permute-start(bf16[128,1024]{1,0:T(8,128)(2,1)S(1)} %section_block.14), channel_id=1, source_target_pairs={{25,0},{29,2},{1,4},{5,6},{2,8},{6,10},{10,12},{14,14},{9,16},{13,... | collective-permute-start | bytes 786440 | tf_op jit(solution)/shard_map/ppermute | solution.py:90
  141.3 63.4 %collective-permute-start.24 = (bf16[384,1024]{1,0:T(8,128)(2,1)S(1)}, bf16[384,1024]{1,0:T(8,128)(2,1)S(1)}, u32[]{:S(2)}, u32[]{:S(2)}) collective-permute-start(bf16[384,1024]{1,0:T(8,128)(2,1)S(1)} %get-tuple-element.12), channel_id=1, source_target_pairs={{29,3},{2,9},{13,19},{18,25}} | collective-permute-start | bytes 2359304 | tf_op jit(solution)/shard_map/ppermute | solution.py:90
  142.0 62.7 %collective-permute-start.19 = (bf16[384,1024]{1,0:T(8,128)(2,1)S(1)}, bf16[384,1024]{1,0:T(8,128)(2,1)S(1)}, u32[]{:S(2)}, u32[]{:S(2)}) collective-permute-start(bf16[384,1024]{1,0:T(8,128)(2,1)S(1)} %get-tuple-element.11), channel_id=1, source_target_pairs={{29,2},{2,8},{13,18},{18,24}} | collective-permute-start | bytes 2359304 | tf_op jit(solution)/shard_map/ppermute | solution.py:90
  142.8 26.3 %collective-permute-start.26 = (bf16[256,1024]{1,0:T(8,128)(2,1)S(1)}, bf16[256,1024]{1,0:T(8,128)(2,1)S(1)}, u32[]{:S(2)}, u32[]{:S(2)}) collective-permute-start(bf16[256,1024]{1,0:T(8,128)(2,1)S(1)} %get-tuple-element.14), channel_id=1, source_target_pairs={{1,1},{2,5},{6,7},{14,11},{9,13},{13,15},{17,17},{18,21},{22,23},{... | collective-permute-start | bytes 1572872 | tf_op jit(solution)/shard_map/ppermute | solution.py:90
  143.5 24.3 %collective-permute-start.30 = (bf16[128,1024]{1,0:T(8,128)(2,1)S(1)}, bf16[128,1024]{1,0:T(8,128)(2,1)S(1)}, u32[]{:S(2)}, u32[]{:S(2)}) collective-permute-start(bf16[128,1024]{1,0:T(8,128)(2,1)S(1)} %collective-permute-done.29.arrived), channel_id=1, source_target_pairs={{1,1},{2,5},{6,7},{14,11},{9,13},{13,15},{17,17},{18,21},{22,23},{... | collective-permute-start | bytes 786440 | tf_op jit(solution)/shard_map/ppermute | solution.py:90
  166.4 38.3 %collective-permute-start.25 = (bf16[256,1024]{1,0:T(8,128)(2,1)S(1)}, bf16[256,1024]{1,0:T(8,128)(2,1)S(1)}, u32[]{:S(2)}, u32[]{:S(2)}) collective-permute-start(bf16[256,1024]{1,0:T(8,128)(2,1)S(1)} %get-tuple-element.13), channel_id=1, source_target_pairs={{1,0},{2,4},{6,6},{14,10},{9,12},{13,14},{17,16},{18,20},{22,22},{... | collective-permute-start | bytes 1572872 | tf_op jit(solution)/shard_map/ppermute | solution.py:90
  167.7 37.0 %collective-permute-start.28 = (bf16[128,1024]{1,0:T(8,128)(2,1)S(1)}, bf16[128,1024]{1,0:T(8,128)(2,1)S(1)}, u32[]{:S(2)}, u32[]{:S(2)}) collective-permute-start(bf16[128,1024]{1,0:T(8,128)(2,1)S(1)} %collective-permute-done.27.arrived), channel_id=1, source_target_pairs={{1,0},{2,4},{6,6},{14,10},{9,12},{13,14},{17,16},{18,20},{22,22},{... | collective-permute-start | bytes 786440 | tf_op jit(solution)/shard_map/ppermute | solution.py:90
  (19 other events, 99.6 us)
where the time goes:
time: 207 us; the launch traced here: 206 us
  waiting for transfers between devices  100 us (48%)
  starting transfers between devices  62.4 us (30%)
  Pallas kernels  30.8 us (15%)
  between operations  6.09 us (3%)
  local copies, waits for them, and re-layouts  5.3 us (3%)
    ppermute x30, waiting for transfers between devices, send(): return lax.ppermute(value, ('section', 'tensor'), pairs)  74.7 us
    ppermute x30, starting transfers between devices, send(): return lax.ppermute(value, ('section', 'tensor'), pairs)  44.8 us
    ppermute x3, waiting for transfers between devices, collapsed(): biases.append(lax.ppermute(in_bias, 'tensor', pairs))  25.4 us
    pallas_call x8, Pallas kernels, run_block(): pl.pallas_call(functools.partial(block_kernel, first_row, len(kept)), out...  24.4 us
    ppermute x3, starting transfers between devices, collapsed(): biases.append(lax.ppermute(in_bias, 'tensor', pairs))  17.6 us
    pallas_call x2, Pallas kernels, assemble(): pl.pallas_call(functools.partial(assemble_kernel, len(own)), out_shape=ja...  4.68 us
  transfers between devices with their start and end apart: 33, of which 6 were waited for; matrix products, arithmetic and copies ran while one was open for 2% of the time, Pallas kernels for 14%

commit v1 on v0

--- a/solution.py
+++ b/solution.py
@@ -72,15 +72,15 @@
             for core in range(2)
         ]
 
-    def crowded(self, section, tensor):
-        return section % 2 == 0 and (tensor >= self.half) != self.side(section)
-
-    def home_pairs(self, slot, shift, crowded=None):
+    def kept_near(self, section, tensor):
+        return section % 2 == 1 and (tensor >= self.half) == self.side(section)
+
+    def home_pairs(self, slot, shift, near=None):
         pairs = []
         for section in range(self.sections):
             for core in range(2):
                 tensor = core * self.half + slot
-                if crowded is None or self.crowded(section, tensor) == crowded:
+                if near is None or self.kept_near(section, tensor) == near:
                     source = self.worker((section - shift) % self.sections, core)
                     pairs.append((source, self.device(section, tensor)))
         return pairs
@@ -118,10 +118,10 @@
     return (widened + total + bias_row).astype(jnp.bfloat16)
 
 
-OWN, FIRST, CROWDED, SLOT = range(4)
-
-
-def block_kernel(first_row, n_kept, flags, arrived, fresh, rows, bias, rows_in, rows_out, *refs):
+OWN, FIRST, NEAR, SLOT = range(4)
+
+
+def block_kernel(first_row, n_kept, box_products, flags, arrived, fresh, rows, bias, rows_in, rows_out, *refs):
     kept, produced, boxes = refs[:n_kept], refs[n_kept], refs[n_kept + 1 :]
     size = arrived.shape[0]
     if first_row is None:
@@ -138,25 +138,19 @@
     result = (widened + total + rows[2:3, :]).astype(jnp.bfloat16)
     produced[...] = result
     if boxes:
-        products, arrivals = boxes
-        earlier = products.shape[0] // size - 1
-        for index in range(earlier):
-            products[index * size : (index + 1) * size, :] = kept[index][...]
-        products[earlier * size :, :] = result
-        for index in range(earlier - 1):
-            arrivals[index * size : (index + 1) * size, :] = kept[earlier + index][...]
-        arrivals[(earlier - 1) * size :, :] = arrived[...]
-
-
-def run_block(first_row, flags, arrived, fresh, operands, products=None, arrivals=None):
+        for index in range(n_kept):
+            boxes[0][index * size : (index + 1) * size, :] = kept[index][...]
+        boxes[0][n_kept * size :, :] = result if box_products else arrived[...]
+
+
+def run_block(first_row, flags, arrived, fresh, operands, kept=(), box_products=False):
     vector = pl.BlockSpec(memory_space=pltpu.VMEM)
-    chunk = lambda count: jax.ShapeDtypeStruct((count * arrived.shape[0],) + arrived.shape[1:], arrived.dtype)
-    shapes, kept = [chunk(1)], []
-    if products is not None:
-        kept = products + arrivals
-        shapes += [chunk(len(products) + 1), chunk(len(arrivals) + 1)]
+    size, width = arrived.shape
+    shapes = [jax.ShapeDtypeStruct((size, width), arrived.dtype)]
+    if kept:
+        shapes.append(jax.ShapeDtypeStruct(((len(kept) + 1) * size, width), arrived.dtype))
     return pl.pallas_call(
-        functools.partial(block_kernel, first_row, len(kept)),
+        functools.partial(block_kernel, first_row, len(kept), box_products),
         out_shape=shapes,
         in_specs=[pl.BlockSpec(memory_space=pltpu.SMEM)] + [vector] * (6 + len(kept)),
         out_specs=[vector] * len(shapes),
@@ -168,7 +162,7 @@
 def collect_kernel(slots, flags, *refs):
     records = refs[-1]
     parts = [refs[index * slots : (index + 1) * slots] for index in range(4)]
-    from_producer, early, late, final = parts
+    near, early, late, final = parts
     size = records.shape[1]
     ticks = records.shape[0]
 
@@ -178,15 +172,16 @@
             value = jnp.where(flags[SLOT] == slot, part[slot][start : start + size, :], value)
         return value
 
-    for tick in range(ticks - 1):
-        own = mine(late, 0) if tick == ticks - 2 else mine(early, tick * size)
-        records[tick] = jnp.where(flags[CROWDED] == 1, mine(from_producer, tick * size), own)
+    for tick in range(ticks - 2):
+        start = tick * size
+        records[tick] = jnp.where(flags[NEAR] == 1, mine(near, start), mine(early, start))
+    records[ticks - 2] = mine(late, 0)
     records[ticks - 1] = mine(final, 0)
 
 
-def collect(flags, from_producer, early, late, final):
+def collect(flags, near, early, late, final):
     vector = pl.BlockSpec(memory_space=pltpu.VMEM)
-    pieces = from_producer + early + late + final
+    pieces = near + early + late + final
     return pl.pallas_call(
         functools.partial(collect_kernel, len(final)),
         out_shape=jax.ShapeDtypeStruct((TICKS,) + final[0].shape, final[0].dtype),
@@ -245,9 +240,9 @@
     own_core = (line + side) % 2
     is_own = core == own_core
     is_first = (line == 0) & (own_core == 0)
-    is_crowded = (core == 0) & (side != line % 2)
+    is_near = (core == 1) & (side != line % 2)
     flags = jnp.stack(
-        [flag.astype(jnp.int32) for flag in (is_own, is_first, is_crowded, tensor_index % half)]
+        [flag.astype(jnp.int32) for flag in (is_own, is_first, is_near, tensor_index % half)]
     )
 
     slots = range(half)
@@ -295,32 +290,36 @@
     full_out = shared(w_out[0], received_out)
     operands = (rows, bias, full_in, full_out)
 
-    def home(values, shift, crowded):
-        return [send(values[slot], places.home_pairs(slot, shift, crowded)) for slot in slots]
+    def home(values, shift, near):
+        return [send(values[slot], places.home_pairs(slot, shift, near)) for slot in slots]
 
     def hop(values):
         return [send(values[slot], places.hop_pairs()) for slot in slots]
 
-    def block(tick_index, slot, *boxes):
+    def blocks(tick_index, *boxes):
         new = waiting if tick_index else currents
         first_row = (tick_index - 1) * chunk if tick_index else None
-        return run_block(first_row, flags, currents[slot], new[slot], operands, *boxes)
-
-    products, arrivals = [[] for _ in slots], [[] for _ in slots]
-    for tick_index in range(TICKS - 2):
+        made = []
         for slot in slots:
-            products[slot] += block(tick_index, slot)
-        currents = hop([made[-1] for made in products])
-        for slot in slots:
-            arrivals[slot].append(currents[slot])
-
-    boxed = [block(TICKS - 2, slot, products[slot], arrivals[slot][:-1]) for slot in slots]
-    currents = hop([box[0] for box in boxed])
-    from_producer = home([box[1] for box in boxed], 1, True)
-    early = home([box[2] for box in boxed], 0, False)
-    late = home(currents, 0, False)
-    final = home([block(TICKS - 1, slot)[0] for slot in slots], 1, None)
-    return collect(flags, from_producer, early, late, final)[None]
+            kept = [boxes[0][slot]] if boxes else []
+            made.append(
+                run_block(first_row, flags, currents[slot], new[slot], operands, kept, *boxes[1:])
+            )
+        return list(zip(*made))
+
+    (products,) = blocks(0)
+    currents = hop(products)
+    arrivals = currents
+    products, boxed = blocks(1, products, True)
+    currents = hop(products)
+    early = home(boxed, 1, False)
+    products, boxed = blocks(2, arrivals, False)
+    currents = hop(products)
+    late = home(products, 1, None)
+    near = home(boxed, 0, True)
+    (products,) = blocks(3)
+    final = home(products, 1, None)
+    return collect(flags, near, early, late, final)[None]
 
 
 def gathered(section_inputs, w_in, in_bias, w_out, out_bias, norm_gain, norm_bias, patches, plan):

time: 207 us -> 192 us (0.928)
  the two profiles are of different devices: /device:TPU:5 before, /device:TPU:0 now
where the time goes in v1:
time: 192 us; the launch traced here: 190 us
  waiting for transfers between devices  82.5 us (43%)
  starting transfers between devices  64.5 us (34%)
  Pallas kernels  30.7 us (16%)
  between operations  5.83 us (3%)
  local copies, waits for them, and re-layouts  5.27 us (3%)
    ppermute x30, waiting for transfers between devices, send(): return lax.ppermute(value, ('section', 'tensor'), pairs)  58.9 us
    ppermute x30, starting transfers between devices, send(): return lax.ppermute(value, ('section', 'tensor'), pairs)  43.6 us
    pallas_call x8, Pallas kernels, run_block(): pl.pallas_call(functools.partial(block_kernel, first_row, len(kept), box_...  24.4 us
    ppermute x3, waiting for transfers between devices, collapsed(): biases.append(lax.ppermute(in_bias, 'tensor', pairs))  23.5 us
    ppermute x3, starting transfers between devices, collapsed(): biases.append(lax.ppermute(in_bias, 'tensor', pairs))  20.9 us
    pallas_call x2, Pallas kernels, assemble(): pl.pallas_call(functools.partial(assemble_kernel, len(own)), out_shape=ja...  4.61 us
  transfers between devices with their start and end apart: 33, of which 6 were waited for; matrix products, arithmetic and copies ran while one was open for 2% of the time, Pallas kernels for 15%

profile of v1, /device:TPU:0, one launch (start us, length us, event | category | flops | bytes accessed | tf_op | source)
XLA Modules:
  0.0 189.7 jit_solution(716038989225019470)
XLA Ops:
  1.7 4.1 %collective-permute-start.13 = (bf16[576,1024]{1,0:T(8,128)(2,1)}, bf16[576,1024]{1,0:T(8,128)(2,1)S(1)}, u32[]{:S(2)}, u32[]{:S(2)}) collective-permute-start(bf16[576,1024]{1,0:T(8,128)(2,1)} %bitcast.18), channel_id=1, source_target_pairs={{3,1},{0,5},{4,6},{5,2},{8,10},{9,14},{15,13},{12,9},{19,17},{16,2... | collective-permute-start | bytes 3538952 | tf_op jit(solution)/shard_map/ppermute | solution.py:90
  6.5 1.7 collective-permute-start.6
  8.2 3.3 %collective-permute-start.2 = (bf16[1,576]{1,0:T(2,128)(2,1)}, bf16[1,576]{1,0:T(2,128)(2,1)S(1)}, u32[]{:S(2)}, u32[]{:S(2)}) collective-permute-start(bf16[1,576]{1,0:T(2,128)(2,1)} %param.11), channel_id=1, source_target_pairs={{1,0},{2,1},{3,2},{0,3},{5,4},{6,5},{7,6},{4,7},{9,8},{10,9},{11,1... | collective-permute-start | bytes 3464 | tf_op jit(solution)/shard_map/ppermute | solution.py:284
  11.5 20.0 %collective-permute-done.2 = bf16[1,576]{1,0:T(2,128)(2,1)S(1)} collective-permute-done((bf16[1,576]{1,0:T(2,128)(2,1)}, bf16[1,576]{1,0:T(2,128)(2,1)S(1)}, u32[]{:S(2)}, u32[]{:S(2)}) %collective-permute-start.2) | collective-permute-done | bytes 1184 | tf_op jit(solution)/shard_map/ppermute | solution.py:284
  31.5 13.8 %collective-permute-start.3 = (bf16[1,576]{1,0:T(2,128)(2,1)}, bf16[1,576]{1,0:T(2,128)(2,1)S(1)}, u32[]{:S(2)}, u32[]{:S(2)}) collective-permute-start(bf16[1,576]{1,0:T(2,128)(2,1)} %param.11), channel_id=1, source_target_pairs={{2,0},{3,1},{0,2},{1,3},{6,4},{7,5},{4,6},{5,7},{10,8},{11,9},{8,1... | collective-permute-start | bytes 3464 | tf_op jit(solution)/shard_map/ppermute | solution.py:284
  45.3 1.8 collective-permute-done.3
  47.1 3.9 %collective-permute-start.4 = (bf16[1,576]{1,0:T(2,128)(2,1)}, bf16[1,576]{1,0:T(2,128)(2,1)S(1)}, u32[]{:S(2)}, u32[]{:S(2)}) collective-permute-start(bf16[1,576]{1,0:T(2,128)(2,1)} %param.11), channel_id=1, source_target_pairs={{3,0},{0,1},{1,2},{2,3},{7,4},{4,5},{5,6},{6,7},{11,8},{8,9},{9,10... | collective-permute-start | bytes 3464 | tf_op jit(solution)/shard_map/ppermute | solution.py:284
  51.0 1.7 collective-permute-done.4
  56.2 7.4 %collective-permute-start.8 = (bf16[576,1024]{1,0:T(8,128)(2,1)}, bf16[576,1024]{1,0:T(8,128)(2,1)S(1)}, u32[]{:S(2)}, u32[]{:S(2)}) collective-permute-start(bf16[576,1024]{1,0:T(8,128)(2,1)} %bitcast.22), channel_id=1, source_target_pairs={{3,1},{0,5},{4,6},{5,2},{8,10},{9,14},{15,13},{12,9},{19,17},{16,2... | collective-permute-start | bytes 3538952 | tf_op jit(solution)/shard_map/ppermute | solution.py:90
  71.8 17.3 %collective-permute-done.8.refs_2_.refs_7_ = bf16[576,1024]{1,0:T(8,128)(2,1)S(1)} collective-permute-done((bf16[576,1024]{1,0:T(8,128)(2,1)}, bf16[576,1024]{1,0:T(8,128)(2,1)S(1)}, u32[]{:S(2)}, u32[]{:S(2)}) %collective-permute-start.8) | collective-permute-done | bytes 1179680 | tf_op jit(solution)/shard_map/ppermute | solution.py:90
  89.1 1.8 collective-permute-start.9
  99.1 4.2 %collective-permute-start = (bf16[128,1024]{1,0:T(8,128)(2,1)S(1)}, bf16[128,1024]{1,0:T(8,128)(2,1)S(1)}, u32[]{:S(2)}, u32[]{:S(2)}) collective-permute-start(bf16[128,1024]{1,0:T(8,128)(2,1)S(1)} %bitcast.26), channel_id=1, source_target_pairs={{0,1},{2,5},{4,2},{6,6},{8,10},{10,14},{12,9},{14,13},{16,17},{18,... | collective-permute-start | bytes 786440 | tf_op jit(solution)/shard_map/ppermute | solution.py:90
  105.5 2.1 %assemble_shards.3.rows_out = bf16[2304,1024]{1,0:T(8,128)(2,1)S(1)} custom-call(s32[4]{0:T(128)S(1)} %pad_add_fusion.flags, bf16[576,1024]{1,0:T(8,128)(2,1)S(1)} %bitcast.20, bf16[576,1024]{1,0:T(8,128)(2,1)} %collective-permute-done.12.refs_1_, bf16[576,1024]{1,0:T(8,128)(2,1)S(1)} %collective-permute-done.13.refs_2_.refs_7_, ...), custom_call_target="tpu_custom_call" | custom-call | tf_op jit(solution)/shard_map/assemble_shards/pallas_call | solution.py:221
  107.7 2.5 %assemble_shards.2.rows_in = bf16[2304,1024]{1,0:T(8,128)(2,1)S(1)} custom-call(s32[4]{0:T(128)S(1)} %pad_add_fusion.flags, bf16[576,1024]{1,0:T(8,128)(2,1)S(1)} %bitcast.24, bf16[576,1024]{1,0:T(8,128)(2,1)} %collective-permute-done.7.refs_1_, bf16[576,1024]{1,0:T(8,128)(2,1)S(1)} %collective-permute-done.8.refs_2_.refs_7_, ...), custom_call_target="tpu_custom_call" | custom-call | tf_op jit(solution)/shard_map/assemble_shards/pallas_call | solution.py:221
  110.2 3.0 %section_block.11.refs_0_ = bf16[128,1024]{1,0:T(8,128)(2,1)S(1)} custom-call(s32[4]{0:T(128)S(1)} %pad_add_fusion.flags, bf16[128,1024]{1,0:T(8,128)(2,1)S(1)} %collective-permute-done.20.arrived.fresh, bf16[128,1024]{1,0:T(8,128)(2,1)S(1)} %collective-permute-done.20.arrived.fresh, f32[3,1024]{1,0:T(4,128)S(1)} %broadcast_select_fusion.1.rows, ...), custom_call_target="tpu_custom_call" | custom-call | tf_op jit(solution)/shard_map/section_block/pallas_call | solution.py:152
  113.9 3.1 %section_block.8.refs_0_ = bf16[128,1024]{1,0:T(8,128)(2,1)S(1)} custom-call(s32[4]{0:T(128)S(1)} %pad_add_fusion.flags, bf16[128,1024]{1,0:T(8,128)(2,1)S(1)} %collective-permute-done.arrived.fresh, bf16[128,1024]{1,0:T(8,128)(2,1)S(1)} %collective-permute-done.arrived.fresh, f32[3,1024]{1,0:T(4,128)S(1)} %broadcast_select_fusion.1.rows, ...), custom_call_target="tpu_custom_call" | custom-call | tf_op jit(solution)/shard_map/section_block/pallas_call | solution.py:152
  117.7 3.1 %section_block.12 = (bf16[128,1024]{1,0:T(8,128)(2,1)S(1)}, bf16[256,1024]{1,0:T(8,128)(2,1)S(1)}) custom-call(s32[4]{0:T(128)S(1)} %pad_add_fusion.flags, bf16[128,1024]{1,0:T(8,128)(2,1)S(1)} %collective-permute-done.21.arrived.refs_0_, bf16[384,1024]{1,0:T(8,128)(2,1)S(1)} %collective-permute-done.22.fresh, f32[3,1024]{1,0:T(4,128)S(1)} %broadcast_select_fusion.1.rows, ...), custom_call_target="tpu_custom_call" | custom-call | tf_op jit(solution)/shard_map/section_block/pallas_call | solution.py:152
  121.5 3.0 %section_block.9 = (bf16[128,1024]{1,0:T(8,128)(2,1)S(1)}, bf16[256,1024]{1,0:T(8,128)(2,1)S(1)}) custom-call(s32[4]{0:T(128)S(1)} %pad_add_fusion.flags, bf16[128,1024]{1,0:T(8,128)(2,1)S(1)} %collective-permute-done.16.arrived.refs_0_, bf16[384,1024]{1,0:T(8,128)(2,1)S(1)} %collective-permute-done.17.fresh, f32[3,1024]{1,0:T(4,128)S(1)} %broadcast_select_fusion.1.rows, ...), custom_call_target="tpu_custom_call" | custom-call | tf_op jit(solution)/shard_map/section_block/pallas_call | solution.py:152
  125.4 3.1 %section_block.13 = (bf16[128,1024]{1,0:T(8,128)(2,1)S(1)}, bf16[256,1024]{1,0:T(8,128)(2,1)S(1)}) custom-call(s32[4]{0:T(128)S(1)} %pad_add_fusion.flags, bf16[128,1024]{1,0:T(8,128)(2,1)S(1)} %collective-permute-done.23.arrived, bf16[384,1024]{1,0:T(8,128)(2,1)S(1)} %collective-permute-done.22.fresh, f32[3,1024]{1,0:T(4,128)S(1)} %broadcast_select_fusion.1.rows, ...), custom_call_target="tpu_custom_call" | custom-call | tf_op jit(solution)/shard_map/section_block/pallas_call | solution.py:152
  129.2 3.1 %section_block.10 = (bf16[128,1024]{1,0:T(8,128)(2,1)S(1)}, bf16[256,1024]{1,0:T(8,128)(2,1)S(1)}) custom-call(s32[4]{0:T(128)S(1)} %pad_add_fusion.flags, bf16[128,1024]{1,0:T(8,128)(2,1)S(1)} %collective-permute-done.18.arrived, bf16[384,1024]{1,0:T(8,128)(2,1)S(1)} %collective-permute-done.17.fresh, f32[3,1024]{1,0:T(4,128)S(1)} %broadcast_select_fusion.1.rows, ...), custom_call_target="tpu_custom_call" | custom-call | tf_op jit(solution)/shard_map/section_block/pallas_call | solution.py:152
  138.3 3.1 %section_block.15 = bf16[128,1024]{1,0:T(8,128)(2,1)S(1)} custom-call(s32[4]{0:T(128)S(1)} %pad_add_fusion.flags, bf16[128,1024]{1,0:T(8,128)(2,1)S(1)} %collective-permute-done.31.arrived, bf16[384,1024]{1,0:T(8,128)(2,1)S(1)} %collective-permute-done.22.fresh, f32[3,1024]{1,0:T(4,128)S(1)} %broadcast_select_fusion.1.rows, ...), custom_call_target="tpu_custom_call" | custom-call | tf_op jit(solution)/shard_map/section_block/pallas_call | solution.py:152
  141.4 3.0 %section_block.14 = bf16[128,1024]{1,0:T(8,128)(2,1)S(1)} custom-call(s32[4]{0:T(128)S(1)} %pad_add_fusion.flags, bf16[128,1024]{1,0:T(8,128)(2,1)S(1)} %collective-permute-done.29.arrived, bf16[384,1024]{1,0:T(8,128)(2,1)S(1)} %collective-permute-done.17.fresh, f32[3,1024]{1,0:T(4,128)S(1)} %broadcast_select_fusion.1.rows, ...), custom_call_target="tpu_custom_call" | custom-call | tf_op jit(solution)/shard_map/section_block/pallas_call | solution.py:152
  144.5 30.8 %collective-permute-done.27.refs_4_ = bf16[128,1024]{1,0:T(8,128)(2,1)S(1)} collective-permute-done((bf16[128,1024]{1,0:T(8,128)(2,1)S(1)}, bf16[128,1024]{1,0:T(8,128)(2,1)S(1)}, u32[]{:S(2)}, u32[]{:S(2)}) %collective-permute-start.27) | collective-permute-done | bytes 262176 | tf_op jit(solution)/shard_map/ppermute | solution.py:90
  177.3 10.8 %collective-permute-done.30.refs_6_ = bf16[128,1024]{1,0:T(8,128)(2,1)S(1)} collective-permute-done((bf16[128,1024]{1,0:T(8,128)(2,1)S(1)}, bf16[128,1024]{1,0:T(8,128)(2,1)S(1)}, u32[]{:S(2)}, u32[]{:S(2)}) %collective-permute-start.30) | collective-permute-done | bytes 262176 | tf_op jit(solution)/shard_map/ppermute | solution.py:90
  (82 shorter events, 32.3 us)
Async XLA Ops:
  0.0 63.6 %collective-permute-start.11 = (bf16[576,1024]{1,0:T(8,128)(2,1)}, bf16[576,1024]{1,0:T(8,128)(2,1)}, u32[]{:S(2)}, u32[]{:S(2)}) collective-permute-start(bf16[576,1024]{1,0:T(8,128)(2,1)} %bitcast.17), channel_id=1, source_target_pairs={{2,5},{7,2},{11,14},{14,9},{18,21},{23,18},{27,30},{30,25}} | collective-permute-start | bytes 3538952 | tf_op jit(solution)/shard_map/ppermute | solution.py:90
  1.7 63.6 %collective-permute-start.13 = (bf16[576,1024]{1,0:T(8,128)(2,1)}, bf16[576,1024]{1,0:T(8,128)(2,1)S(1)}, u32[]{:S(2)}, u32[]{:S(2)}) collective-permute-start(bf16[576,1024]{1,0:T(8,128)(2,1)} %bitcast.18), channel_id=1, source_target_pairs={{3,1},{0,5},{4,6},{5,2},{8,10},{9,14},{15,13},{12,9},{19,17},{16,2... | collective-permute-start | bytes 3538952 | tf_op jit(solution)/shard_map/ppermute | solution.py:90
  5.8 61.2 %collective-permute-start.15 = (bf16[576,1024]{1,0:T(8,128)(2,1)}, bf16[576,1024]{1,0:T(8,128)(2,1)S(1)}, u32[]{:S(2)}, u32[]{:S(2)}) collective-permute-start(bf16[576,1024]{1,0:T(8,128)(2,1)} %bitcast.19), channel_id=1, source_target_pairs={{1,5},{6,2},{10,14},{13,9},{17,21},{22,18},{26,30},{29,25}} | collective-permute-start | bytes 3538952 | tf_op jit(solution)/shard_map/ppermute | solution.py:90
  6.5 62.2 %collective-permute-start.6 = (bf16[576,1024]{1,0:T(8,128)(2,1)}, bf16[576,1024]{1,0:T(8,128)(2,1)}, u32[]{:S(2)}, u32[]{:S(2)}) collective-permute-start(bf16[576,1024]{1,0:T(8,128)(2,1)} %bitcast.21), channel_id=1, source_target_pairs={{2,5},{7,2},{11,14},{14,9},{18,21},{23,18},{27,30},{30,25}} | collective-permute-start | bytes 3538952 | tf_op jit(solution)/shard_map/ppermute | solution.py:90
  8.2 23.3 %collective-permute-start.2 = (bf16[1,576]{1,0:T(2,128)(2,1)}, bf16[1,576]{1,0:T(2,128)(2,1)S(1)}, u32[]{:S(2)}, u32[]{:S(2)}) collective-permute-start(bf16[1,576]{1,0:T(2,128)(2,1)} %param.11), channel_id=1, source_target_pairs={{1,0},{2,1},{3,2},{0,3},{5,4},{6,5},{7,6},{4,7},{9,8},{10,9},{11,1... | collective-permute-start | bytes 3464 | tf_op jit(solution)/shard_map/ppermute | solution.py:284
  31.5 15.5 %collective-permute-start.3 = (bf16[1,576]{1,0:T(2,128)(2,1)}, bf16[1,576]{1,0:T(2,128)(2,1)S(1)}, u32[]{:S(2)}, u32[]{:S(2)}) collective-permute-start(bf16[1,576]{1,0:T(2,128)(2,1)} %param.11), channel_id=1, source_target_pairs={{2,0},{3,1},{0,2},{1,3},{6,4},{7,5},{4,6},{5,7},{10,8},{11,9},{8,1... | collective-permute-start | bytes 3464 | tf_op jit(solution)/shard_map/ppermute | solution.py:284
  47.1 5.6 %collective-permute-start.4 = (bf16[1,576]{1,0:T(2,128)(2,1)}, bf16[1,576]{1,0:T(2,128)(2,1)S(1)}, u32[]{:S(2)}, u32[]{:S(2)}) collective-permute-start(bf16[1,576]{1,0:T(2,128)(2,1)} %param.11), channel_id=1, source_target_pairs={{3,0},{0,1},{1,2},{2,3},{7,4},{4,5},{5,6},{6,7},{11,8},{8,9},{9,10... | collective-permute-start | bytes 3464 | tf_op jit(solution)/shard_map/ppermute | solution.py:284
  56.2 32.9 %collective-permute-start.8 = (bf16[576,1024]{1,0:T(8,128)(2,1)}, bf16[576,1024]{1,0:T(8,128)(2,1)S(1)}, u32[]{:S(2)}, u32[]{:S(2)}) collective-permute-start(bf16[576,1024]{1,0:T(8,128)(2,1)} %bitcast.22), channel_id=1, source_target_pairs={{3,1},{0,5},{4,6},{5,2},{8,10},{9,14},{15,13},{12,9},{19,17},{16,2... | collective-permute-start | bytes 3538952 | tf_op jit(solution)/shard_map/ppermute | solution.py:90
  63.6 34.0 %collective-permute-start.10 = (bf16[576,1024]{1,0:T(8,128)(2,1)}, bf16[576,1024]{1,0:T(8,128)(2,1)}, u32[]{:S(2)}, u32[]{:S(2)}) collective-permute-start(bf16[576,1024]{1,0:T(8,128)(2,1)} %bitcast.23), channel_id=1, source_target_pairs={{1,5},{6,2},{10,14},{13,9},{17,21},{22,18},{26,30},{29,25}} | collective-permute-start | bytes 3538952 | tf_op jit(solution)/shard_map/ppermute | solution.py:90
  65.3 33.8 %collective-permute-start.12 = (bf16[576,1024]{1,0:T(8,128)(2,1)}, bf16[576,1024]{1,0:T(8,128)(2,1)}, u32[]{:S(2)}, u32[]{:S(2)}) collective-permute-start(bf16[576,1024]{1,0:T(8,128)(2,1)} %collective-permute-done.11.refs_5_), channel_id=1, source_target_pairs={{5,1},{2,6},{14,10},{9,13},{21,17},{18,22},{30,26},{25,29}} | collective-permute-start | bytes 3538952 | tf_op jit(solution)/shard_map/ppermute | solution.py:90
  68.0 35.3 %collective-permute-start.14 = (bf16[576,1024]{1,0:T(8,128)(2,1)S(1)}, bf16[576,1024]{1,0:T(8,128)(2,1)S(1)}, u32[]{:S(2)}, u32[]{:S(2)}) collective-permute-start(bf16[576,1024]{1,0:T(8,128)(2,1)S(1)} %collective-permute-done.13.refs_2_.refs_7_), channel_id=1, source_target_pairs={{1,5},{5,1},{2,6},{6,2},{10,14},{14,10},{9,13},{13,9},{17,21},{21,... | collective-permute-start | bytes 3538952 | tf_op jit(solution)/shard_map/ppermute | solution.py:90
  68.7 35.3 %collective-permute-start.7 = (bf16[576,1024]{1,0:T(8,128)(2,1)}, bf16[576,1024]{1,0:T(8,128)(2,1)}, u32[]{:S(2)}, u32[]{:S(2)}) collective-permute-start(bf16[576,1024]{1,0:T(8,128)(2,1)} %collective-permute-done.6.refs_5_), channel_id=1, source_target_pairs={{5,1},{2,6},{14,10},{9,13},{21,17},{18,22},{30,26},{25,29}} | collective-permute-start | bytes 3538952 | tf_op jit(solution)/shard_map/ppermute | solution.py:90
  89.1 18.6 %collective-permute-start.9 = (bf16[576,1024]{1,0:T(8,128)(2,1)S(1)}, bf16[576,1024]{1,0:T(8,128)(2,1)}, u32[]{:S(2)}, u32[]{:S(2)}) collective-permute-start(bf16[576,1024]{1,0:T(8,128)(2,1)S(1)} %collective-permute-done.8.refs_2_.refs_7_), channel_id=1, source_target_pairs={{1,5},{5,1},{2,6},{6,2},{10,14},{14,10},{9,13},{13,9},{17,21},{21,... | collective-permute-start | bytes 3538952 | tf_op jit(solution)/shard_map/ppermute | solution.py:90
  98.4 11.8 %collective-permute-start.20 = (bf16[128,1024]{1,0:T(8,128)(2,1)S(1)}, bf16[128,1024]{1,0:T(8,128)(2,1)S(1)}, u32[]{:S(2)}, u32[]{:S(2)}) collective-permute-start(bf16[128,1024]{1,0:T(8,128)(2,1)S(1)} %bitcast.25), channel_id=1, source_target_pairs={{1,1},{3,5},{5,2},{7,6},{9,10},{11,14},{13,9},{15,13},{17,17},{19,... | collective-permute-start | bytes 786440 | tf_op jit(solution)/shard_map/ppermute | solution.py:90
  99.1 14.9 %collective-permute-start = (bf16[128,1024]{1,0:T(8,128)(2,1)S(1)}, bf16[128,1024]{1,0:T(8,128)(2,1)S(1)}, u32[]{:S(2)}, u32[]{:S(2)}) collective-permute-start(bf16[128,1024]{1,0:T(8,128)(2,1)S(1)} %bitcast.26), channel_id=1, source_target_pairs={{0,1},{2,5},{4,2},{6,6},{8,10},{10,14},{12,9},{14,13},{16,17},{18,... | collective-permute-start | bytes 786440 | tf_op jit(solution)/shard_map/ppermute | solution.py:90
  103.3 14.4 %collective-permute-start.22 = (bf16[384,1024]{1,0:T(8,128)(2,1)S(1)}, bf16[384,1024]{1,0:T(8,128)(2,1)S(1)}, u32[]{:S(2)}, u32[]{:S(2)}) collective-permute-start(bf16[384,1024]{1,0:T(8,128)(2,1)S(1)} %pad_maximum_fusion), channel_id=1, source_target_pairs={{1,1},{3,5}} | collective-permute-start | bytes 2359304 | tf_op jit(solution)/shard_map/ppermute | solution.py:90
  104.1 17.4 %collective-permute-start.17 = (bf16[384,1024]{1,0:T(8,128)(2,1)S(1)}, bf16[384,1024]{1,0:T(8,128)(2,1)S(1)}, u32[]{:S(2)}, u32[]{:S(2)}) collective-permute-start(bf16[384,1024]{1,0:T(8,128)(2,1)S(1)} %pad_maximum_fusion), channel_id=1, source_target_pairs={{0,1},{2,5}} | collective-permute-start | bytes 2359304 | tf_op jit(solution)/shard_map/ppermute | solution.py:90
  128.5 7.1 %collective-permute-start.31 = (bf16[128,1024]{1,0:T(8,128)(2,1)S(1)}, bf16[128,1024]{1,0:T(8,128)(2,1)S(1)}, u32[]{:S(2)}, u32[]{:S(2)}) collective-permute-start(bf16[128,1024]{1,0:T(8,128)(2,1)S(1)} %get-tuple-element.20), channel_id=1, source_target_pairs={{1,2},{5,6},{2,10},{6,14},{10,9},{14,13},{9,17},{13,21},{17,18},{2... | collective-permute-start | bytes 786440 | tf_op jit(solution)/shard_map/ppermute | solution.py:90
  132.9 43.0 %collective-permute-start.26 = (bf16[256,1024]{1,0:T(8,128)(2,1)S(1)}, bf16[256,1024]{1,0:T(8,128)(2,1)S(1)}, u32[]{:S(2)}, u32[]{:S(2)}) collective-permute-start(bf16[256,1024]{1,0:T(8,128)(2,1)S(1)} %get-tuple-element.18), channel_id=1, source_target_pairs={{25,1},{29,3},{1,5},{2,9},{6,11},{14,15},{9,17},{13,19},{17,21},{1... | collective-permute-start | bytes 1572872 | tf_op jit(solution)/shard_map/ppermute | solution.py:90
  134.3 42.9 %collective-permute-start.25 = (bf16[256,1024]{1,0:T(8,128)(2,1)S(1)}, bf16[256,1024]{1,0:T(8,128)(2,1)S(1)}, u32[]{:S(2)}, u32[]{:S(2)}) collective-permute-start(bf16[256,1024]{1,0:T(8,128)(2,1)S(1)} %get-tuple-element.17), channel_id=1, source_target_pairs={{25,0},{29,2},{1,4},{2,8},{6,10},{14,14},{9,16},{13,18},{17,20},{1... | collective-permute-start | bytes 1572872 | tf_op jit(solution)/shard_map/ppermute | solution.py:90
  135.6 39.6 %collective-permute-start.27 = (bf16[128,1024]{1,0:T(8,128)(2,1)S(1)}, bf16[128,1024]{1,0:T(8,128)(2,1)S(1)}, u32[]{:S(2)}, u32[]{:S(2)}) collective-permute-start(bf16[128,1024]{1,0:T(8,128)(2,1)S(1)} %get-tuple-element.19), channel_id=1, source_target_pairs={{25,0},{29,2},{1,4},{5,6},{2,8},{6,10},{10,12},{14,14},{9,16},{13,... | collective-permute-start | bytes 786440 | tf_op jit(solution)/shard_map/ppermute | solution.py:90
  136.9 51.1 %collective-permute-start.24 = (bf16[256,1024]{1,0:T(8,128)(2,1)S(1)}, bf16[256,1024]{1,0:T(8,128)(2,1)S(1)}, u32[]{:S(2)}, u32[]{:S(2)}) collective-permute-start(bf16[256,1024]{1,0:T(8,128)(2,1)S(1)} %get-tuple-element.16), channel_id=1, source_target_pairs={{6,7},{9,13},{22,23},{25,29}} | collective-permute-start | bytes 1572872 | tf_op jit(solution)/shard_map/ppermute | solution.py:90
  137.6 50.4 %collective-permute-start.19 = (bf16[256,1024]{1,0:T(8,128)(2,1)S(1)}, bf16[256,1024]{1,0:T(8,128)(2,1)S(1)}, u32[]{:S(2)}, u32[]{:S(2)}) collective-permute-start(bf16[256,1024]{1,0:T(8,128)(2,1)S(1)} %get-tuple-element.14), channel_id=1, source_target_pairs={{6,6},{9,12},{22,22},{25,28}} | collective-permute-start | bytes 1572872 | tf_op jit(solution)/shard_map/ppermute | solution.py:90
  175.9 12.1 %collective-permute-start.30 = (bf16[128,1024]{1,0:T(8,128)(2,1)S(1)}, bf16[128,1024]{1,0:T(8,128)(2,1)S(1)}, u32[]{:S(2)}, u32[]{:S(2)}) collective-permute-start(bf16[128,1024]{1,0:T(8,128)(2,1)S(1)} %section_block.14), channel_id=1, source_target_pairs={{25,0},{29,2},{1,4},{5,6},{2,8},{6,10},{10,12},{14,14},{9,16},{13,... | collective-permute-start | bytes 786440 | tf_op jit(solution)/shard_map/ppermute | solution.py:90
  (19 other events, 86.2 us)

commit v2 on v1

--- a/solution.py
+++ b/solution.py
@@ -51,9 +51,12 @@
         ]
         return [(target, source) for source, target in pairs] if back else pairs
 
+    def quarter(self, core, slot):
+        return self.tensors - 1 - slot if core else slot
+
     def token_pairs(self, slot, sections):
         return [
-            (self.device(section, core * self.half + slot), self.worker(section, core))
+            (self.device(section, self.quarter(core, slot)), self.worker(section, core))
             for section in sections
             for core in range(2)
         ]
@@ -79,11 +82,24 @@
         pairs = []
         for section in range(self.sections):
             for core in range(2):
-                tensor = core * self.half + slot
+                tensor = self.quarter(core, slot)
                 if near is None or self.kept_near(section, tensor) == near:
                     source = self.worker((section - shift) % self.sections, core)
                     pairs.append((source, self.device(section, tensor)))
         return pairs
+
+
+    def marks(self):
+        table = []
+        for section in range(self.sections):
+            for tensor in range(self.tensors):
+                side = int(tensor >= self.half)
+                own = (section // 2 + side) % 2
+                slot = self.tensors - 1 - tensor if side else tensor
+                first = section < 2 and own == 0
+                near = self.kept_near(section, tensor)
+                table.append([float(mark) for mark in (section % 2 == own, first, near, slot)])
+        return table
 
 
 def send(value, pairs):
@@ -118,24 +134,69 @@
     return (widened + total + bias_row).astype(jnp.bfloat16)
 
 
-OWN, FIRST, NEAR, SLOT = range(4)
-
-
-def block_kernel(first_row, n_kept, box_products, flags, arrived, fresh, rows, bias, rows_in, rows_out, *refs):
+GAIN, SHIFT, BIAS, OWN, FIRST, NEAR, SLOT = range(7)
+
+
+def row(rows, index):
+    return rows[index : index + 1, :]
+
+
+def mark(rows, index):
+    return jnp.max(row(rows, index))
+
+
+def enter_kernel(arrived, rows, bias, rows_in, hidden):
+    normed, _ = normalize(arrived[...], row(rows, GAIN), row(rows, SHIFT))
+    preact = lax.dot_general(
+        normed, rows_in[...], (((1,), (1,)), ((), ())), preferred_element_type=jnp.float32
+    )
+    hidden[...] = activate(preact + bias[...]).astype(jnp.bfloat16)
+
+
+def leave_kernel(arrived, hidden, rows, rows_out, produced):
+    total = jnp.dot(hidden[...], rows_out[...], preferred_element_type=jnp.float32)
+    widened = arrived[...].astype(jnp.float32)
+    produced[...] = (widened + total + row(rows, BIAS)).astype(jnp.bfloat16)
+
+
+def enter(arrived, rows, bias, full_in):
+    vector = pl.BlockSpec(memory_space=pltpu.VMEM)
+    return pl.pallas_call(
+        enter_kernel,
+        out_shape=jax.ShapeDtypeStruct((arrived.shape[0], full_in.shape[0]), jnp.bfloat16),
+        in_specs=[vector] * 4,
+        out_specs=vector,
+        compiler_params=pltpu.CompilerParams(vmem_limit_bytes=8 * 2**20),
+        name="enter_block",
+    )(arrived, rows, bias, full_in)
+
+
+def leave(arrived, hidden, rows, full_out):
+    vector = pl.BlockSpec(memory_space=pltpu.VMEM)
+    return pl.pallas_call(
+        leave_kernel,
+        out_shape=jax.ShapeDtypeStruct(arrived.shape, arrived.dtype),
+        in_specs=[vector] * 4,
+        out_specs=vector,
+        compiler_params=pltpu.CompilerParams(vmem_limit_bytes=8 * 2**20),
+        name="leave_block",
+    )(arrived, hidden, rows, full_out)
+
+
+def block_kernel(
+    first_row, n_kept, box_products, arrived, fresh, rows, bias, rows_in, rows_out, *refs
+):
     kept, produced, boxes = refs[:n_kept], refs[n_kept], refs[n_kept + 1 :]
     size = arrived.shape[0]
-    if first_row is None:
-        current = arrived[...]
-    else:
-        new = fresh[first_row : first_row + size, :]
-        current = jnp.where(flags[FIRST] == 1, new, arrived[...])
-    normed, widened = normalize(current, rows[0:1, :], rows[1:2, :])
+    new = fresh[first_row : first_row + size, :].astype(jnp.float32)
+    current = jnp.where(row(rows, FIRST) == 1.0, new, arrived[...].astype(jnp.float32))
+    normed, widened = normalize(current, row(rows, GAIN), row(rows, SHIFT))
     preact = lax.dot_general(
         normed, rows_in[...], (((1,), (1,)), ((), ())), preferred_element_type=jnp.float32
     )
     hidden = activate(preact + bias[...]).astype(jnp.bfloat16)
     total = jnp.dot(hidden, rows_out[...], preferred_element_type=jnp.float32)
-    result = (widened + total + rows[2:3, :]).astype(jnp.bfloat16)
+    result = (widened + total + row(rows, BIAS)).astype(jnp.bfloat16)
     produced[...] = result
     if boxes:
         for index in range(n_kept):
@@ -143,7 +204,7 @@
         boxes[0][n_kept * size :, :] = result if box_products else arrived[...]
 
 
-def run_block(first_row, flags, arrived, fresh, operands, kept=(), box_products=False):
+def run_block(first_row, arrived, fresh, operands, kept=(), box_products=False):
     vector = pl.BlockSpec(memory_space=pltpu.VMEM)
     size, width = arrived.shape
     shapes = [jax.ShapeDtypeStruct((size, width), arrived.dtype)]
@@ -152,47 +213,48 @@
     return pl.pallas_call(
         functools.partial(block_kernel, first_row, len(kept), box_products),
         out_shape=shapes,
-        in_specs=[pl.BlockSpec(memory_space=pltpu.SMEM)] + [vector] * (6 + len(kept)),
+        in_specs=[vector] * (6 + len(kept)),
         out_specs=[vector] * len(shapes),
         compiler_params=pltpu.CompilerParams(vmem_limit_bytes=8 * 2**20),
         name="section_block",
-    )(flags, arrived, fresh, *operands, *kept)
-
-
-def collect_kernel(slots, flags, *refs):
+    )(arrived, fresh, *operands, *kept)
+
+
+def collect_kernel(slots, rows, *refs):
     records = refs[-1]
     parts = [refs[index * slots : (index + 1) * slots] for index in range(4)]
     near, early, late, final = parts
     size = records.shape[1]
     ticks = records.shape[0]
+    choice, is_near = mark(rows, SLOT), mark(rows, NEAR)
 
     def mine(part, start):
         value = part[0][start : start + size, :]
         for slot in range(1, slots):
-            value = jnp.where(flags[SLOT] == slot, part[slot][start : start + size, :], value)
+            value = jnp.where(choice == slot, part[slot][start : start + size, :], value)
         return value
 
     for tick in range(ticks - 2):
         start = tick * size
-        records[tick] = jnp.where(flags[NEAR] == 1, mine(near, start), mine(early, start))
+        records[tick] = jnp.where(is_near == 1.0, mine(near, start), mine(early, start))
     records[ticks - 2] = mine(late, 0)
     records[ticks - 1] = mine(final, 0)
 
 
-def collect(flags, near, early, late, final):
+def collect(rows, near, early, late, final):
     vector = pl.BlockSpec(memory_space=pltpu.VMEM)
     pieces = near + early + late + final
     return pl.pallas_call(
         functools.partial(collect_kernel, len(final)),
         out_shape=jax.ShapeDtypeStruct((TICKS,) + final[0].shape, final[0].dtype),
-        in_specs=[pl.BlockSpec(memory_space=pltpu.SMEM)] + [vector] * len(pieces),
+        in_specs=[vector] * (1 + len(pieces)),
         out_specs=vector,
         compiler_params=pltpu.CompilerParams(vmem_limit_bytes=8 * 2**20),
         name="collect_quarters",
-    )(flags, *pieces)
-
-
-def assemble_kernel(count, flags, *refs):
+    )(rows, *pieces)
+
+
+def assemble_kernel(count, rows, *refs):
     own, other, full, done = refs[:count], refs[count : 2 * count], refs[-2], refs[-1]
     size = own[0].shape[0]
 
@@ -206,44 +268,39 @@
         for copy in copies:
             copy.wait()
 
-    @pl.when(flags[OWN] == 1)
+    is_own = mark(rows, OWN)
+
+    @pl.when(is_own == 1.0)
     def _():
         place(own)
 
-    @pl.when(flags[OWN] == 0)
+    @pl.when(is_own != 1.0)
     def _():
         place(other)
 
 
-def assemble(flags, own, other):
+def assemble(rows, own, other):
+    vector = pl.BlockSpec(memory_space=pltpu.VMEM)
     main = pl.BlockSpec(memory_space=pltpu.MemorySpace.HBM)
     size, width = own[0].shape
     return pl.pallas_call(
         functools.partial(assemble_kernel, len(own)),
         out_shape=jax.ShapeDtypeStruct((size * len(own), width), own[0].dtype),
-        in_specs=[pl.BlockSpec(memory_space=pltpu.SMEM)] + [main] * (2 * len(own)),
-        out_specs=pl.BlockSpec(memory_space=pltpu.VMEM),
+        in_specs=[vector] + [main] * (2 * len(own)),
+        out_specs=vector,
         scratch_shapes=[pltpu.SemaphoreType.DMA((len(own),))],
         compiler_params=pltpu.CompilerParams(vmem_limit_bytes=8 * 2**20),
         name="assemble_shards",
-    )(flags, *own, *other)
+    )(rows, *own, *other)
 
 
 def collapsed(section_inputs, w_in, in_bias, w_out, out_bias, norm_gain, norm_bias, patches, plan):
     places = Plan(lax.axis_size("section"), lax.axis_size("tensor"))
     tensors, half = places.tensors, places.half
-    section_index = lax.axis_index("section")
-    tensor_index = lax.axis_index("tensor")
-    core = section_index % 2
-    line = section_index // 2
-    side = (tensor_index >= half).astype(jnp.int32)
-    own_core = (line + side) % 2
-    is_own = core == own_core
-    is_first = (line == 0) & (own_core == 0)
-    is_near = (core == 1) & (side != line % 2)
-    flags = jnp.stack(
-        [flag.astype(jnp.int32) for flag in (is_own, is_first, is_near, tensor_index % half)]
-    )
+    place = lax.axis_index("section") * tensors + lax.axis_index("tensor")
+    marks = lax.dynamic_slice_in_dim(jnp.array(places.marks(), jnp.float32), place, 1, 0)
+    marks = jnp.broadcast_to(marks[0][:, None], (marks.shape[1], norm_gain.shape[1]))
+    is_own = marks[0, 0] == 1.0
 
     slots = range(half)
     chunk = section_inputs.shape[1]
@@ -261,7 +318,7 @@
             swapped = send(received[slot], partner)
             own += [received[slot], swapped]
             other += [swapped, received[slot]]
-        return assemble(flags, own, other)
+        return assemble(rows, own, other)
 
     def tokens(value, sections):
         return [send(value, places.token_pairs(slot, sections)) for slot in slots]
@@ -280,13 +337,15 @@
 
     biases = [in_bias]
     for step in range(1, tensors):
-        pairs = [((place + step) % tensors, place) for place in range(tensors)]
+        pairs = [((to + step) % tensors, to) for to in range(tensors)]
         biases.append(lax.ppermute(in_bias, "tensor", pairs))
     bias = jnp.concatenate(biases, axis=1).astype(jnp.float32)
     rows = jnp.concatenate([norm_gain, norm_bias, out_bias], axis=0)
     bias = jnp.where(is_own, bias, send(bias, partner))
     rows = jnp.where(is_own, rows, send(rows, partner))
+    rows = jnp.concatenate([rows, marks], axis=0)
     full_in = shared(w_in[0], received_in)
+    hiddens = [enter(currents[slot], rows, bias, full_in) for slot in slots]
     full_out = shared(w_out[0], received_out)
     operands = (rows, bias, full_in, full_out)
 
@@ -297,17 +356,16 @@
         return [send(values[slot], places.hop_pairs()) for slot in slots]
 
     def blocks(tick_index, *boxes):
-        new = waiting if tick_index else currents
-        first_row = (tick_index - 1) * chunk if tick_index else None
+        first_row = (tick_index - 1) * chunk
         made = []
         for slot in slots:
             kept = [boxes[0][slot]] if boxes else []
             made.append(
-                run_block(first_row, flags, currents[slot], new[slot], operands, kept, *boxes[1:])
+                run_block(first_row, currents[slot], waiting[slot], operands, kept, *boxes[1:])
             )
         return list(zip(*made))
 
-    (products,) = blocks(0)
+    products = [leave(currents[slot], hiddens[slot], rows, full_out) for slot in slots]
     currents = hop(products)
     arrivals = currents
     products, boxed = blocks(1, products, True)
@@ -319,7 +377,7 @@
     near = home(boxed, 0, True)
     (products,) = blocks(3)
     final = home(products, 1, None)
-    return collect(flags, near, early, late, final)[None]
+    return collect(rows, near, early, late, final)[None]
 
 
 def gathered(section_inputs, w_in, in_bias, w_out, out_bias, norm_gain, norm_bias, patches, plan):

time: 192 us -> 176 us (0.917)
  starting transfers between devices: 64.5 us -> 53.8 us
  Pallas kernels: 30.7 us -> 24.7 us
    ppermute x3, starting transfers between devices: 20.9 us -> 11.2 us  [collapsed(): biases.append(lax.ppermute(in_bias, 'tensor', pairs))]
    pallas_call x8 -> x6, Pallas kernels: 24.4 us -> 15.2 us  [run_block(): pl.pallas_call(functools.partial(block_kernel, first_row, len(kept), box_...]
    pallas_call x0 -> x4, Pallas kernels: none -> 5.38 us  [the longest x2 3.78 us: enter(): pl.pallas_call(enter_kernel, out_shape=jax.ShapeDtypeStruct((arrived.shap...]
  transfers between devices with their start and end apart: 33 -> 33, of which waited for: 6 -> 7; matrix products, arithmetic and copies ran while one was open for 2% -> 3% of each run, Pallas kernels for 15% -> 13%
where the time goes in v2:
time: 176 us; the launch traced here: 175 us
  waiting for transfers between devices  82.5 us (47%)
  starting transfers between devices  53.8 us (31%)
  Pallas kernels  24.7 us (14%)
  between operations  6.51 us (4%)
  local copies, waits for them, and re-layouts  6.06 us (3%)
    ppermute x30, waiting for transfers between devices, send(): return lax.ppermute(value, ('section', 'tensor'), pairs)  58.1 us
    ppermute x30, starting transfers between devices, send(): return lax.ppermute(value, ('section', 'tensor'), pairs)  42.6 us
    ppermute x3, waiting for transfers between devices, collapsed(): biases.append(lax.ppermute(in_bias, 'tensor', pairs))  24.4 us
    pallas_call x6, Pallas kernels, run_block(): pl.pallas_call(functools.partial(block_kernel, first_row, len(kept), box_...  15.2 us
    ppermute x3, starting transfers between devices, collapsed(): biases.append(lax.ppermute(in_bias, 'tensor', pairs))  11.2 us
    pallas_call x2, Pallas kernels, enter(): pl.pallas_call(enter_kernel, out_shape=jax.ShapeDtypeStruct((arrived.shap...  3.78 us
  transfers between devices with their start and end apart: 33, of which 7 were waited for; matrix products, arithmetic and copies ran while one was open for 3% of the time, Pallas kernels for 13%

profile of v2, /device:TPU:0, one launch (start us, length us, event | category | flops | bytes accessed | tf_op | source)
XLA Modules:
  0.0 174.5 jit_solution(7712202767495238433)
XLA Ops:
  0.0 1.7 collective-permute-start.6
  1.7 4.0 %collective-permute-start.8 = (bf16[576,1024]{1,0:T(8,128)(2,1)}, bf16[576,1024]{1,0:T(8,128)(2,1)S(1)}, u32[]{:S(2)}, u32[]{:S(2)}) collective-permute-start(bf16[576,1024]{1,0:T(8,128)(2,1)} %bitcast.18), channel_id=1, source_target_pairs={{3,1},{0,5},{4,6},{5,2},{8,10},{9,14},{15,13},{12,9},{19,17},{16,2... | collective-permute-start | bytes 3538952 | tf_op jit(solution)/shard_map/ppermute | solution.py:106
  7.2 3.4 %collective-permute-start.2 = (bf16[1,576]{1,0:T(2,128)(2,1)}, bf16[1,576]{1,0:T(2,128)(2,1)S(1)}, u32[]{:S(2)}, u32[]{:S(2)}) collective-permute-start(bf16[1,576]{1,0:T(2,128)(2,1)} %param.12), channel_id=1, source_target_pairs={{1,0},{2,1},{3,2},{0,3},{5,4},{6,5},{7,6},{4,7},{9,8},{10,9},{11,1... | collective-permute-start | bytes 3464 | tf_op jit(solution)/shard_map/ppermute | solution.py:341
  10.6 20.9 %collective-permute-done.2 = bf16[1,576]{1,0:T(2,128)(2,1)S(1)} collective-permute-done((bf16[1,576]{1,0:T(2,128)(2,1)}, bf16[1,576]{1,0:T(2,128)(2,1)S(1)}, u32[]{:S(2)}, u32[]{:S(2)}) %collective-permute-start.2) | collective-permute-done | bytes 1184 | tf_op jit(solution)/shard_map/ppermute | solution.py:341
  31.5 4.0 %collective-permute-start.3 = (bf16[1,576]{1,0:T(2,128)(2,1)}, bf16[1,576]{1,0:T(2,128)(2,1)S(1)}, u32[]{:S(2)}, u32[]{:S(2)}) collective-permute-start(bf16[1,576]{1,0:T(2,128)(2,1)} %param.12), channel_id=1, source_target_pairs={{2,0},{3,1},{0,2},{1,3},{6,4},{7,5},{4,6},{5,7},{10,8},{11,9},{8,1... | collective-permute-start | bytes 3464 | tf_op jit(solution)/shard_map/ppermute | solution.py:341
  35.5 1.8 %collective-permute-done.3 = bf16[1,576]{1,0:T(2,128)(2,1)S(1)} collective-permute-done((bf16[1,576]{1,0:T(2,128)(2,1)}, bf16[1,576]{1,0:T(2,128)(2,1)S(1)}, u32[]{:S(2)}, u32[]{:S(2)}) %collective-permute-start.3) | collective-permute-done | bytes 1184 | tf_op jit(solution)/shard_map/ppermute | solution.py:341
  37.3 3.9 %collective-permute-start.4 = (bf16[1,576]{1,0:T(2,128)(2,1)}, bf16[1,576]{1,0:T(2,128)(2,1)S(1)}, u32[]{:S(2)}, u32[]{:S(2)}) collective-permute-start(bf16[1,576]{1,0:T(2,128)(2,1)} %param.12), channel_id=1, source_target_pairs={{3,0},{0,1},{1,2},{2,3},{7,4},{4,5},{5,6},{6,7},{11,8},{8,9},{9,10... | collective-permute-start | bytes 3464 | tf_op jit(solution)/shard_map/ppermute | solution.py:341
  41.1 1.7 collective-permute-done.4
  46.4 1.7 collective-permute-start.11
  48.8 7.0 %collective-permute-start.13 = (bf16[576,1024]{1,0:T(8,128)(2,1)}, bf16[576,1024]{1,0:T(8,128)(2,1)S(1)}, u32[]{:S(2)}, u32[]{:S(2)}) collective-permute-start(bf16[576,1024]{1,0:T(8,128)(2,1)} %bitcast.22), channel_id=1, source_target_pairs={{3,1},{0,5},{4,6},{5,2},{8,10},{9,14},{15,13},{12,9},{19,17},{16,2... | collective-permute-start | bytes 3538952 | tf_op jit(solution)/shard_map/ppermute | solution.py:106
  55.8 1.7 collective-permute-start.15
  70.5 11.1 %collective-permute-done.13.refs_2_.refs_7_ = bf16[576,1024]{1,0:T(8,128)(2,1)S(1)} collective-permute-done((bf16[576,1024]{1,0:T(8,128)(2,1)}, bf16[576,1024]{1,0:T(8,128)(2,1)S(1)}, u32[]{:S(2)}, u32[]{:S(2)}) %collective-permute-start.13) | collective-permute-done | bytes 1179680 | tf_op jit(solution)/shard_map/ppermute | solution.py:106
  83.9 5.5 %collective-permute-start.17 = (bf16[384,1024]{1,0:T(8,128)(2,1)S(1)}, bf16[384,1024]{1,0:T(8,128)(2,1)S(1)}, u32[]{:S(2)}, u32[]{:S(2)}) collective-permute-start(bf16[384,1024]{1,0:T(8,128)(2,1)S(1)} %pad_maximum_fusion), channel_id=1, source_target_pairs={{0,1},{3,5}} | collective-permute-start | bytes 2359304 | tf_op jit(solution)/shard_map/ppermute | solution.py:106
  92.7 1.9 %enter_block.3.hidden = bf16[128,2304]{1,0:T(8,128)(2,1)S(1)} custom-call(bf16[128,1024]{1,0:T(8,128)(2,1)S(1)} %copy-done.5, f32[7,1024]{1,0:T(8,128)S(1)} %pad_maximum_fusion.1.rows, f32[1,2304]{1,0:T(1,128)S(1)} %broadcast_select_fusion.bias, bf16[2304,1024]{1,0:T(8,128)(2,1)S(1)} %assemble_shards.2.rows_in), custom_call_target="tpu_custom_call" | custom-call | tf_op jit(solution)/shard_map/enter_block/pallas_call | solution.py:164
  97.2 7.3 %collective-permute-done.1.arrived = bf16[128,1024]{1,0:T(8,128)(2,1)S(1)} collective-permute-done((bf16[128,1024]{1,0:T(8,128)(2,1)S(1)}, bf16[128,1024]{1,0:T(8,128)(2,1)S(1)}, u32[]{:S(2)}, u32[]{:S(2)}) %collective-permute-start.1) | collective-permute-done | bytes 262176 | tf_op jit(solution)/shard_map/ppermute | solution.py:106
  104.5 1.9 %enter_block.2.hidden = bf16[128,2304]{1,0:T(8,128)(2,1)S(1)} custom-call(bf16[128,1024]{1,0:T(8,128)(2,1)S(1)} %collective-permute-done.1.arrived, f32[7,1024]{1,0:T(8,128)S(1)} %pad_maximum_fusion.1.rows, f32[1,2304]{1,0:T(1,128)S(1)} %broadcast_select_fusion.bias, bf16[2304,1024]{1,0:T(8,128)(2,1)S(1)} %assemble_shards.2.rows_in), custom_call_target="tpu_custom_call" | custom-call | tf_op jit(solution)/shard_map/enter_block/pallas_call | solution.py:164
  107.9 2.5 %section_block.8 = (bf16[128,1024]{1,0:T(8,128)(2,1)S(1)}, bf16[256,1024]{1,0:T(8,128)(2,1)S(1)}) custom-call(bf16[128,1024]{1,0:T(8,128)(2,1)S(1)} %collective-permute-done.21.arrived.refs_0_, bf16[384,1024]{1,0:T(8,128)(2,1)S(1)} %collective-permute-done.22.fresh, f32[7,1024]{1,0:T(8,128)S(1)} %pad_maximum_fusion.1.rows, ...), custom_call_target="tpu_custom_call" | custom-call | tf_op jit(solution)/shard_map/section_block/pallas_call | solution.py:213
  111.1 2.5 %section_block.6 = (bf16[128,1024]{1,0:T(8,128)(2,1)S(1)}, bf16[256,1024]{1,0:T(8,128)(2,1)S(1)}) custom-call(bf16[128,1024]{1,0:T(8,128)(2,1)S(1)} %collective-permute-done.16.arrived.refs_0_, bf16[384,1024]{1,0:T(8,128)(2,1)S(1)} %collective-permute-done.17.fresh, f32[7,1024]{1,0:T(8,128)S(1)} %pad_maximum_fusion.1.rows, ...), custom_call_target="tpu_custom_call" | custom-call | tf_op jit(solution)/shard_map/section_block/pallas_call | solution.py:213
  114.6 2.5 %section_block.9 = (bf16[128,1024]{1,0:T(8,128)(2,1)S(1)}, bf16[256,1024]{1,0:T(8,128)(2,1)S(1)}) custom-call(bf16[128,1024]{1,0:T(8,128)(2,1)S(1)} %collective-permute-done.23.arrived, bf16[384,1024]{1,0:T(8,128)(2,1)S(1)} %collective-permute-done.22.fresh, f32[7,1024]{1,0:T(8,128)S(1)} %pad_maximum_fusion.1.rows, f32[1,2304]{1,0:T(1,128)S(1)} %broadcast_select_fusion.bias, ...), custom_call_target="tpu_custom_call" | custom-call | tf_op jit(solution)/shard_map/section_block/pallas_call | solution.py:213
  117.8 2.5 %section_block.7 = (bf16[128,1024]{1,0:T(8,128)(2,1)S(1)}, bf16[256,1024]{1,0:T(8,128)(2,1)S(1)}) custom-call(bf16[128,1024]{1,0:T(8,128)(2,1)S(1)} %collective-permute-done.18.arrived, bf16[384,1024]{1,0:T(8,128)(2,1)S(1)} %collective-permute-done.17.fresh, f32[7,1024]{1,0:T(8,128)S(1)} %pad_maximum_fusion.1.rows, f32[1,2304]{1,0:T(1,128)S(1)} %broadcast_select_fusion.bias, ...), custom_call_target="tpu_custom_call" | custom-call | tf_op jit(solution)/shard_map/section_block/pallas_call | solution.py:213
  126.4 2.5 %section_block.11 = bf16[128,1024]{1,0:T(8,128)(2,1)S(1)} custom-call(bf16[128,1024]{1,0:T(8,128)(2,1)S(1)} %collective-permute-done.31.arrived, bf16[384,1024]{1,0:T(8,128)(2,1)S(1)} %collective-permute-done.22.fresh, f32[7,1024]{1,0:T(8,128)S(1)} %pad_maximum_fusion.1.rows, f32[1,2304]{1,0:T(1,128)S(1)} %broadcast_select_fusion.bias, ...), custom_call_target="tpu_custom_call" | custom-call | tf_op jit(solution)/shard_map/section_block/pallas_call | solution.py:213
  129.0 2.5 %section_block.10 = bf16[128,1024]{1,0:T(8,128)(2,1)S(1)} custom-call(bf16[128,1024]{1,0:T(8,128)(2,1)S(1)} %collective-permute-done.29.arrived, bf16[384,1024]{1,0:T(8,128)(2,1)S(1)} %collective-permute-done.17.fresh, f32[7,1024]{1,0:T(8,128)S(1)} %pad_maximum_fusion.1.rows, f32[1,2304]{1,0:T(1,128)S(1)} %broadcast_select_fusion.bias, ...), custom_call_target="tpu_custom_call" | custom-call | tf_op jit(solution)/shard_map/section_block/pallas_call | solution.py:213
  131.5 28.4 %collective-permute-done.27.refs_4_ = bf16[128,1024]{1,0:T(8,128)(2,1)S(1)} collective-permute-done((bf16[128,1024]{1,0:T(8,128)(2,1)S(1)}, bf16[128,1024]{1,0:T(8,128)(2,1)S(1)}, u32[]{:S(2)}, u32[]{:S(2)}) %collective-permute-start.27) | collective-permute-done | bytes 262176 | tf_op jit(solution)/shard_map/ppermute | solution.py:106
  161.9 11.3 %collective-permute-done.30.refs_6_ = bf16[128,1024]{1,0:T(8,128)(2,1)S(1)} collective-permute-done((bf16[128,1024]{1,0:T(8,128)(2,1)S(1)}, bf16[128,1024]{1,0:T(8,128)(2,1)S(1)}, u32[]{:S(2)}, u32[]{:S(2)}) %collective-permute-start.30) | collective-permute-done | bytes 262176 | tf_op jit(solution)/shard_map/ppermute | solution.py:106
  (90 shorter events, 33.6 us)
Async XLA Ops:
  0.0 55.8 %collective-permute-start.6 = (bf16[576,1024]{1,0:T(8,128)(2,1)}, bf16[576,1024]{1,0:T(8,128)(2,1)}, u32[]{:S(2)}, u32[]{:S(2)}) collective-permute-start(bf16[576,1024]{1,0:T(8,128)(2,1)} %bitcast.17), channel_id=1, source_target_pairs={{2,5},{7,2},{11,14},{14,9},{18,21},{23,18},{27,30},{30,25}} | collective-permute-start | bytes 3538952 | tf_op jit(solution)/shard_map/ppermute | solution.py:106
  1.7 55.8 %collective-permute-start.8 = (bf16[576,1024]{1,0:T(8,128)(2,1)}, bf16[576,1024]{1,0:T(8,128)(2,1)S(1)}, u32[]{:S(2)}, u32[]{:S(2)}) collective-permute-start(bf16[576,1024]{1,0:T(8,128)(2,1)} %bitcast.18), channel_id=1, source_target_pairs={{3,1},{0,5},{4,6},{5,2},{8,10},{9,14},{15,13},{12,9},{19,17},{16,2... | collective-permute-start | bytes 3538952 | tf_op jit(solution)/shard_map/ppermute | solution.py:106
  5.8 53.4 %collective-permute-start.10 = (bf16[576,1024]{1,0:T(8,128)(2,1)}, bf16[576,1024]{1,0:T(8,128)(2,1)S(1)}, u32[]{:S(2)}, u32[]{:S(2)}) collective-permute-start(bf16[576,1024]{1,0:T(8,128)(2,1)} %bitcast.19), channel_id=1, source_target_pairs={{1,5},{6,2},{10,14},{13,9},{17,21},{22,18},{26,30},{29,25}} | collective-permute-start | bytes 3538952 | tf_op jit(solution)/shard_map/ppermute | solution.py:106
  6.5 41.6 %collective-permute-start.20 = (bf16[128,1024]{1,0:T(8,128)(2,1)}, bf16[128,1024]{1,0:T(8,128)(2,1)S(1)}, u32[]{:S(2)}, u32[]{:S(2)}) collective-permute-start(bf16[128,1024]{1,0:T(8,128)(2,1)} %bitcast.26), channel_id=1, source_target_pairs={{1,1},{2,5},{5,2},{6,6},{9,10},{10,14},{13,9},{14,13},{17,17},{18,... | collective-permute-start | bytes 786440 | tf_op jit(solution)/shard_map/ppermute | solution.py:106
  7.2 24.3 %collective-permute-start.2 = (bf16[1,576]{1,0:T(2,128)(2,1)}, bf16[1,576]{1,0:T(2,128)(2,1)S(1)}, u32[]{:S(2)}, u32[]{:S(2)}) collective-permute-start(bf16[1,576]{1,0:T(2,128)(2,1)} %param.12), channel_id=1, source_target_pairs={{1,0},{2,1},{3,2},{0,3},{5,4},{6,5},{7,6},{4,7},{9,8},{10,9},{11,1... | collective-permute-start | bytes 3464 | tf_op jit(solution)/shard_map/ppermute | solution.py:341
  31.5 5.8 %collective-permute-start.3 = (bf16[1,576]{1,0:T(2,128)(2,1)}, bf16[1,576]{1,0:T(2,128)(2,1)S(1)}, u32[]{:S(2)}, u32[]{:S(2)}) collective-permute-start(bf16[1,576]{1,0:T(2,128)(2,1)} %param.12), channel_id=1, source_target_pairs={{2,0},{3,1},{0,2},{1,3},{6,4},{7,5},{4,6},{5,7},{10,8},{11,9},{8,1... | collective-permute-start | bytes 3464 | tf_op jit(solution)/shard_map/ppermute | solution.py:341
  46.4 23.2 %collective-permute-start.11 = (bf16[576,1024]{1,0:T(8,128)(2,1)}, bf16[576,1024]{1,0:T(8,128)(2,1)}, u32[]{:S(2)}, u32[]{:S(2)}) collective-permute-start(bf16[576,1024]{1,0:T(8,128)(2,1)} %bitcast.21), channel_id=1, source_target_pairs={{2,5},{7,2},{11,14},{14,9},{18,21},{23,18},{27,30},{30,25}} | collective-permute-start | bytes 3538952 | tf_op jit(solution)/shard_map/ppermute | solution.py:106
  48.8 32.8 %collective-permute-start.13 = (bf16[576,1024]{1,0:T(8,128)(2,1)}, bf16[576,1024]{1,0:T(8,128)(2,1)S(1)}, u32[]{:S(2)}, u32[]{:S(2)}) collective-permute-start(bf16[576,1024]{1,0:T(8,128)(2,1)} %bitcast.22), channel_id=1, source_target_pairs={{3,1},{0,5},{4,6},{5,2},{8,10},{9,14},{15,13},{12,9},{19,17},{16,2... | collective-permute-start | bytes 3538952 | tf_op jit(solution)/shard_map/ppermute | solution.py:106
  55.8 27.4 %collective-permute-start.15 = (bf16[576,1024]{1,0:T(8,128)(2,1)}, bf16[576,1024]{1,0:T(8,128)(2,1)}, u32[]{:S(2)}, u32[]{:S(2)}) collective-permute-start(bf16[576,1024]{1,0:T(8,128)(2,1)} %bitcast.23), channel_id=1, source_target_pairs={{1,5},{6,2},{10,14},{13,9},{17,21},{22,18},{26,30},{29,25}} | collective-permute-start | bytes 3538952 | tf_op jit(solution)/shard_map/ppermute | solution.py:106
  57.5 26.4 %collective-permute-start.7 = (bf16[576,1024]{1,0:T(8,128)(2,1)}, bf16[576,1024]{1,0:T(8,128)(2,1)}, u32[]{:S(2)}, u32[]{:S(2)}) collective-permute-start(bf16[576,1024]{1,0:T(8,128)(2,1)} %collective-permute-done.6.refs_5_), channel_id=1, source_target_pairs={{5,1},{2,6},{14,10},{9,13},{21,17},{18,22},{30,26},{25,29}} | collective-permute-start | bytes 3538952 | tf_op jit(solution)/shard_map/ppermute | solution.py:106
  60.2 29.3 %collective-permute-start.9 = (bf16[576,1024]{1,0:T(8,128)(2,1)S(1)}, bf16[576,1024]{1,0:T(8,128)(2,1)S(1)}, u32[]{:S(2)}, u32[]{:S(2)}) collective-permute-start(bf16[576,1024]{1,0:T(8,128)(2,1)S(1)} %collective-permute-done.8.refs_2_.refs_7_), channel_id=1, source_target_pairs={{1,5},{5,1},{2,6},{6,2},{10,14},{14,10},{9,13},{13,9},{17,21},{21,... | collective-permute-start | bytes 3538952 | tf_op jit(solution)/shard_map/ppermute | solution.py:106
  69.6 24.9 %collective-permute-start.12 = (bf16[576,1024]{1,0:T(8,128)(2,1)}, bf16[576,1024]{1,0:T(8,128)(2,1)S(1)}, u32[]{:S(2)}, u32[]{:S(2)}) collective-permute-start(bf16[576,1024]{1,0:T(8,128)(2,1)} %collective-permute-done.11.refs_5_), channel_id=1, source_target_pairs={{5,1},{2,6},{14,10},{9,13},{21,17},{18,22},{30,26},{25,29}} | collective-permute-start | bytes 3538952 | tf_op jit(solution)/shard_map/ppermute | solution.py:106
  81.6 13.0 %collective-permute-start.14 = (bf16[576,1024]{1,0:T(8,128)(2,1)S(1)}, bf16[576,1024]{1,0:T(8,128)(2,1)S(1)}, u32[]{:S(2)}, u32[]{:S(2)}) collective-permute-start(bf16[576,1024]{1,0:T(8,128)(2,1)S(1)} %collective-permute-done.13.refs_2_.refs_7_), channel_id=1, source_target_pairs={{1,5},{5,1},{2,6},{6,2},{10,14},{14,10},{9,13},{13,9},{17,21},{21,... | collective-permute-start | bytes 3538952 | tf_op jit(solution)/shard_map/ppermute | solution.py:106
  83.2 24.7 %collective-permute-start.22 = (bf16[384,1024]{1,0:T(8,128)(2,1)S(1)}, bf16[384,1024]{1,0:T(8,128)(2,1)S(1)}, u32[]{:S(2)}, u32[]{:S(2)}) collective-permute-start(bf16[384,1024]{1,0:T(8,128)(2,1)S(1)} %pad_maximum_fusion), channel_id=1, source_target_pairs={{1,1},{2,5}} | collective-permute-start | bytes 2359304 | tf_op jit(solution)/shard_map/ppermute | solution.py:106
  83.9 27.2 %collective-permute-start.17 = (bf16[384,1024]{1,0:T(8,128)(2,1)S(1)}, bf16[384,1024]{1,0:T(8,128)(2,1)S(1)}, u32[]{:S(2)}, u32[]{:S(2)}) collective-permute-start(bf16[384,1024]{1,0:T(8,128)(2,1)S(1)} %pad_maximum_fusion), channel_id=1, source_target_pairs={{0,1},{3,5}} | collective-permute-start | bytes 2359304 | tf_op jit(solution)/shard_map/ppermute | solution.py:106
  89.5 15.0 %collective-permute-start.1 = (bf16[128,1024]{1,0:T(8,128)(2,1)S(1)}, bf16[128,1024]{1,0:T(8,128)(2,1)S(1)}, u32[]{:S(2)}, u32[]{:S(2)}) collective-permute-start(bf16[128,1024]{1,0:T(8,128)(2,1)S(1)} %bitcast.27), channel_id=1, source_target_pairs={{0,1},{3,5},{4,2},{7,6},{8,10},{11,14},{12,9},{15,13},{16,17},{19,... | collective-permute-start | bytes 786440 | tf_op jit(solution)/shard_map/ppermute | solution.py:106
  96.5 11.4 %collective-permute-start.21 = (bf16[128,1024]{1,0:T(8,128)(2,1)S(1)}, bf16[128,1024]{1,0:T(8,128)(2,1)S(1)}, u32[]{:S(2)}, u32[]{:S(2)}) collective-permute-start(bf16[128,1024]{1,0:T(8,128)(2,1)S(1)} %leave_block.3.refs_0_), channel_id=1, source_target_pairs={{1,2},{5,6},{2,10},{6,14},{10,9},{14,13},{9,17},{13,21},{17,18},{2... | collective-permute-start | bytes 786440 | tf_op jit(solution)/shard_map/ppermute | solution.py:106
  117.1 6.6 %collective-permute-start.31 = (bf16[128,1024]{1,0:T(8,128)(2,1)S(1)}, bf16[128,1024]{1,0:T(8,128)(2,1)S(1)}, u32[]{:S(2)}, u32[]{:S(2)}) collective-permute-start(bf16[128,1024]{1,0:T(8,128)(2,1)S(1)} %get-tuple-element.20), channel_id=1, source_target_pairs={{1,2},{5,6},{2,10},{6,14},{10,9},{14,13},{9,17},{13,21},{17,18},{2... | collective-permute-start | bytes 786440 | tf_op jit(solution)/shard_map/ppermute | solution.py:106
  121.0 39.6 %collective-permute-start.26 = (bf16[256,1024]{1,0:T(8,128)(2,1)S(1)}, bf16[256,1024]{1,0:T(8,128)(2,1)S(1)}, u32[]{:S(2)}, u32[]{:S(2)}) collective-permute-start(bf16[256,1024]{1,0:T(8,128)(2,1)S(1)} %get-tuple-element.18), channel_id=1, source_target_pairs={{25,1},{29,2},{1,5},{2,9},{6,10},{14,14},{9,17},{13,18},{17,21},{1... | collective-permute-start | bytes 1572872 | tf_op jit(solution)/shard_map/ppermute | solution.py:106
  122.4 39.5 %collective-permute-start.25 = (bf16[256,1024]{1,0:T(8,128)(2,1)S(1)}, bf16[256,1024]{1,0:T(8,128)(2,1)S(1)}, u32[]{:S(2)}, u32[]{:S(2)}) collective-permute-start(bf16[256,1024]{1,0:T(8,128)(2,1)S(1)} %get-tuple-element.17), channel_id=1, source_target_pairs={{25,0},{29,3},{1,4},{2,8},{6,11},{14,15},{9,16},{13,19},{17,20},{1... | collective-permute-start | bytes 1572872 | tf_op jit(solution)/shard_map/ppermute | solution.py:106
  123.7 36.2 %collective-permute-start.27 = (bf16[128,1024]{1,0:T(8,128)(2,1)S(1)}, bf16[128,1024]{1,0:T(8,128)(2,1)S(1)}, u32[]{:S(2)}, u32[]{:S(2)}) collective-permute-start(bf16[128,1024]{1,0:T(8,128)(2,1)S(1)} %get-tuple-element.19), channel_id=1, source_target_pairs={{25,0},{29,3},{1,4},{5,7},{2,8},{6,11},{10,12},{14,15},{9,16},{13,... | collective-permute-start | bytes 786440 | tf_op jit(solution)/shard_map/ppermute | solution.py:106
  125.0 48.2 %collective-permute-start.24 = (bf16[256,1024]{1,0:T(8,128)(2,1)S(1)}, bf16[256,1024]{1,0:T(8,128)(2,1)S(1)}, u32[]{:S(2)}, u32[]{:S(2)}) collective-permute-start(bf16[256,1024]{1,0:T(8,128)(2,1)S(1)} %get-tuple-element.16), channel_id=1, source_target_pairs={{6,6},{9,13},{22,22},{25,29}} | collective-permute-start | bytes 1572872 | tf_op jit(solution)/shard_map/ppermute | solution.py:106
  125.7 47.5 %collective-permute-start.19 = (bf16[256,1024]{1,0:T(8,128)(2,1)S(1)}, bf16[256,1024]{1,0:T(8,128)(2,1)S(1)}, u32[]{:S(2)}, u32[]{:S(2)}) collective-permute-start(bf16[256,1024]{1,0:T(8,128)(2,1)S(1)} %get-tuple-element.14), channel_id=1, source_target_pairs={{6,7},{9,12},{22,23},{25,28}} | collective-permute-start | bytes 1572872 | tf_op jit(solution)/shard_map/ppermute | solution.py:106
  160.6 12.6 %collective-permute-start.30 = (bf16[128,1024]{1,0:T(8,128)(2,1)S(1)}, bf16[128,1024]{1,0:T(8,128)(2,1)S(1)}, u32[]{:S(2)}, u32[]{:S(2)}) collective-permute-start(bf16[128,1024]{1,0:T(8,128)(2,1)S(1)} %section_block.10), channel_id=1, source_target_pairs={{25,0},{29,3},{1,4},{5,7},{2,8},{6,11},{10,12},{14,15},{9,16},{13,... | collective-permute-start | bytes 786440 | tf_op jit(solution)/shard_map/ppermute | solution.py:106
  (21 other events, 187.6 us)

commit v3 on v2

--- a/solution.py
+++ b/solution.py
@@ -183,10 +183,7 @@
     )(arrived, hidden, rows, full_out)
 
 
-def block_kernel(
-    first_row, n_kept, box_products, arrived, fresh, rows, bias, rows_in, rows_out, *refs
-):
-    kept, produced, boxes = refs[:n_kept], refs[n_kept], refs[n_kept + 1 :]
+def block_kernel(first_row, arrived, fresh, rows, bias, rows_in, rows_out, *refs):
     size = arrived.shape[0]
     new = fresh[first_row : first_row + size, :].astype(jnp.float32)
     current = jnp.where(row(rows, FIRST) == 1.0, new, arrived[...].astype(jnp.float32))
@@ -197,21 +194,24 @@
     hidden = activate(preact + bias[...]).astype(jnp.bfloat16)
     total = jnp.dot(hidden, rows_out[...], preferred_element_type=jnp.float32)
     result = (widened + total + row(rows, BIAS)).astype(jnp.bfloat16)
+    if len(refs) == 1:
+        refs[0][...] = result
+        return
+    product, arrival, produced, products, arrivals = refs
     produced[...] = result
-    if boxes:
-        for index in range(n_kept):
-            boxes[0][index * size : (index + 1) * size, :] = kept[index][...]
-        boxes[0][n_kept * size :, :] = result if box_products else arrived[...]
-
-
-def run_block(first_row, arrived, fresh, operands, kept=(), box_products=False):
+    products[:size, :] = product[...]
+    products[size:, :] = result
+    arrivals[:size, :] = arrival[...]
+    arrivals[size:, :] = arrived[...]
+
+
+def run_block(first_row, arrived, fresh, operands, kept=()):
     vector = pl.BlockSpec(memory_space=pltpu.VMEM)
     size, width = arrived.shape
-    shapes = [jax.ShapeDtypeStruct((size, width), arrived.dtype)]
-    if kept:
-        shapes.append(jax.ShapeDtypeStruct(((len(kept) + 1) * size, width), arrived.dtype))
+    chunks = [1, 2, 2] if kept else [1]
+    shapes = [jax.ShapeDtypeStruct((count * size, width), arrived.dtype) for count in chunks]
     return pl.pallas_call(
-        functools.partial(block_kernel, first_row, len(kept), box_products),
+        functools.partial(block_kernel, first_row),
         out_shape=shapes,
         in_specs=[vector] * (6 + len(kept)),
         out_specs=[vector] * len(shapes),
@@ -222,8 +222,8 @@
 
 def collect_kernel(slots, rows, *refs):
     records = refs[-1]
-    parts = [refs[index * slots : (index + 1) * slots] for index in range(4)]
-    near, early, late, final = parts
+    parts = [refs[index * slots : (index + 1) * slots] for index in range(5)]
+    early, late, near, near_late, final = parts
     size = records.shape[1]
     ticks = records.shape[0]
     choice, is_near = mark(rows, SLOT), mark(rows, NEAR)
@@ -234,16 +234,18 @@
             value = jnp.where(choice == slot, part[slot][start : start + size, :], value)
         return value
 
-    for tick in range(ticks - 2):
-        start = tick * size
-        records[tick] = jnp.where(is_near == 1.0, mine(near, start), mine(early, start))
-    records[ticks - 2] = mine(late, 0)
+    def either(tick, far, far_start, close, close_start):
+        records[tick] = jnp.where(is_near == 1.0, mine(close, close_start), mine(far, far_start))
+
+    either(0, early, 0, near, 0)
+    either(1, late, 0, near, size)
+    either(2, late, size, near_late, 0)
     records[ticks - 1] = mine(final, 0)
 
 
-def collect(rows, near, early, late, final):
+def collect(rows, early, late, near, near_late, final):
     vector = pl.BlockSpec(memory_space=pltpu.VMEM)
-    pieces = near + early + late + final
+    pieces = early + late + near + near_late + final
     return pl.pallas_call(
         functools.partial(collect_kernel, len(final)),
         out_shape=jax.ShapeDtypeStruct((TICKS,) + final[0].shape, final[0].dtype),
@@ -355,29 +357,28 @@
     def hop(values):
         return [send(values[slot], places.hop_pairs()) for slot in slots]
 
-    def blocks(tick_index, *boxes):
+    def blocks(tick_index, *kept):
         first_row = (tick_index - 1) * chunk
         made = []
         for slot in slots:
-            kept = [boxes[0][slot]] if boxes else []
-            made.append(
-                run_block(first_row, currents[slot], waiting[slot], operands, kept, *boxes[1:])
-            )
+            chunks = [array[slot] for array in kept]
+            made.append(run_block(first_row, currents[slot], waiting[slot], operands, chunks))
         return list(zip(*made))
 
     products = [leave(currents[slot], hiddens[slot], rows, full_out) for slot in slots]
     currents = hop(products)
+    early = home(products, 1, False)
     arrivals = currents
-    products, boxed = blocks(1, products, True)
+    (products,) = blocks(1)
     currents = hop(products)
-    early = home(boxed, 1, False)
-    products, boxed = blocks(2, arrivals, False)
-    currents = hop(products)
-    late = home(products, 1, None)
-    near = home(boxed, 0, True)
+    made, boxed_products, boxed_arrivals = blocks(2, products, arrivals)
+    currents = hop(made)
+    late = home(boxed_products, 1, False)
+    near = home(boxed_arrivals, 0, True)
+    near_late = home(currents, 0, True)
     (products,) = blocks(3)
     final = home(products, 1, None)
-    return collect(rows, near, early, late, final)[None]
+    return collect(rows, early, late, near, near_late, final)[None]
 
 
 def gathered(section_inputs, w_in, in_bias, w_out, out_bias, norm_gain, norm_bias, patches, plan):

time: 176 us -> 177 us (level)
  the two profiles are of different devices: /device:TPU:0 before, /device:TPU:3 now
where the time goes in v3:
time: 177 us; the launch traced here: 176 us
  waiting for transfers between devices  82.6 us (47%)
  starting transfers between devices  55.5 us (31%)
  Pallas kernels  24.7 us (14%)
  between operations  6.54 us (4%)
  local copies, waits for them, and re-layouts  6.06 us (3%)
    ppermute x32, waiting for transfers between devices, send(): return lax.ppermute(value, ('section', 'tensor'), pairs)  59.4 us
    ppermute x32, starting transfers between devices, send(): return lax.ppermute(value, ('section', 'tensor'), pairs)  45.8 us
    ppermute x3, waiting for transfers between devices, collapsed(): biases.append(lax.ppermute(in_bias, 'tensor', pairs))  23.2 us
    pallas_call x6, Pallas kernels, run_block(): pl.pallas_call(functools.partial(block_kernel, first_row), out_shape=shap...  15.1 us
    ppermute x3, starting transfers between devices, collapsed(): biases.append(lax.ppermute(in_bias, 'tensor', pairs))  9.73 us
    pallas_call x2, Pallas kernels, enter(): pl.pallas_call(enter_kernel, out_shape=jax.ShapeDtypeStruct((arrived.shap...  3.78 us
  transfers between devices with their start and end apart: 35, of which 6 were waited for; matrix products, arithmetic and copies ran while one was open for 3% of the time, Pallas kernels for 13%

profile of v3, /device:TPU:3, one launch (start us, length us, event | category | flops | bytes accessed | tf_op | source)
XLA Modules:
  0.0 176.3 jit_solution(9977893080418176388)
XLA Ops:
  0.0 1.7 collective-permute-start.6
  1.7 3.4 %collective-permute-start.8 = (bf16[576,1024]{1,0:T(8,128)(2,1)}, bf16[576,1024]{1,0:T(8,128)(2,1)S(1)}, u32[]{:S(2)}, u32[]{:S(2)}) collective-permute-start(bf16[576,1024]{1,0:T(8,128)(2,1)} %bitcast.18), channel_id=1, source_target_pairs={{3,1},{0,5},{4,6},{5,2},{8,10},{9,14},{15,13},{12,9},{19,17},{16,2... | collective-permute-start | bytes 3538952 | tf_op jit(solution)/shard_map/ppermute | solution.py:106
  6.6 2.0 %collective-permute-start.2 = (bf16[1,576]{1,0:T(2,128)(2,1)}, bf16[1,576]{1,0:T(2,128)(2,1)S(1)}, u32[]{:S(2)}, u32[]{:S(2)}) collective-permute-start(bf16[1,576]{1,0:T(2,128)(2,1)} %param.12), channel_id=1, source_target_pairs={{1,0},{2,1},{3,2},{0,3},{5,4},{6,5},{7,6},{4,7},{9,8},{10,9},{11,1... | collective-permute-start | bytes 3464 | tf_op jit(solution)/shard_map/ppermute | solution.py:343
  8.6 20.6 %collective-permute-done.2 = bf16[1,576]{1,0:T(2,128)(2,1)S(1)} collective-permute-done((bf16[1,576]{1,0:T(2,128)(2,1)}, bf16[1,576]{1,0:T(2,128)(2,1)S(1)}, u32[]{:S(2)}, u32[]{:S(2)}) %collective-permute-start.2) | collective-permute-done | bytes 1184 | tf_op jit(solution)/shard_map/ppermute | solution.py:343
  29.1 4.7 %collective-permute-start.3 = (bf16[1,576]{1,0:T(2,128)(2,1)}, bf16[1,576]{1,0:T(2,128)(2,1)S(1)}, u32[]{:S(2)}, u32[]{:S(2)}) collective-permute-start(bf16[1,576]{1,0:T(2,128)(2,1)} %param.12), channel_id=1, source_target_pairs={{2,0},{3,1},{0,2},{1,3},{6,4},{7,5},{4,6},{5,7},{10,8},{11,9},{8,1... | collective-permute-start | bytes 3464 | tf_op jit(solution)/shard_map/ppermute | solution.py:343
  35.1 3.0 %collective-permute-start.4 = (bf16[1,576]{1,0:T(2,128)(2,1)}, bf16[1,576]{1,0:T(2,128)(2,1)S(1)}, u32[]{:S(2)}, u32[]{:S(2)}) collective-permute-start(bf16[1,576]{1,0:T(2,128)(2,1)} %param.12), channel_id=1, source_target_pairs={{3,0},{0,1},{1,2},{2,3},{7,4},{4,5},{5,6},{6,7},{11,8},{8,9},{9,10... | collective-permute-start | bytes 3464 | tf_op jit(solution)/shard_map/ppermute | solution.py:343
  38.1 1.4 collective-permute-done.4
  43.0 1.7 collective-permute-start.11
  45.4 7.3 %collective-permute-start.13 = (bf16[576,1024]{1,0:T(8,128)(2,1)}, bf16[576,1024]{1,0:T(8,128)(2,1)S(1)}, u32[]{:S(2)}, u32[]{:S(2)}) collective-permute-start(bf16[576,1024]{1,0:T(8,128)(2,1)} %bitcast.22), channel_id=1, source_target_pairs={{3,1},{0,5},{4,6},{5,2},{8,10},{9,14},{15,13},{12,9},{19,17},{16,2... | collective-permute-start | bytes 3538952 | tf_op jit(solution)/shard_map/ppermute | solution.py:106
  52.7 1.7 collective-permute-start.15
  54.4 1.7 collective-permute-start.7
  67.4 9.7 %collective-permute-done.13.refs_2_.refs_7_ = bf16[576,1024]{1,0:T(8,128)(2,1)S(1)} collective-permute-done((bf16[576,1024]{1,0:T(8,128)(2,1)}, bf16[576,1024]{1,0:T(8,128)(2,1)S(1)}, u32[]{:S(2)}, u32[]{:S(2)}) %collective-permute-start.13) | collective-permute-done | bytes 1179680 | tf_op jit(solution)/shard_map/ppermute | solution.py:106
  80.1 8.3 %collective-permute-start.1 = (bf16[128,1024]{1,0:T(8,128)(2,1)S(1)}, bf16[128,1024]{1,0:T(8,128)(2,1)S(1)}, u32[]{:S(2)}, u32[]{:S(2)}) collective-permute-start(bf16[128,1024]{1,0:T(8,128)(2,1)S(1)} %bitcast.27), channel_id=1, source_target_pairs={{0,1},{3,5},{4,2},{7,6},{8,10},{11,14},{12,9},{15,13},{16,17},{19,... | collective-permute-start | bytes 786440 | tf_op jit(solution)/shard_map/ppermute | solution.py:106
  88.6 1.7 assemble_shards.2.rows_in
  90.3 1.9 %enter_block.3.hidden = bf16[128,2304]{1,0:T(8,128)(2,1)S(1)} custom-call(bf16[128,1024]{1,0:T(8,128)(2,1)S(1)} %copy-done.5, f32[7,1024]{1,0:T(8,128)S(1)} %pad_maximum_fusion.1.rows, f32[1,2304]{1,0:T(1,128)S(1)} %broadcast_select_fusion.bias, bf16[2304,1024]{1,0:T(8,128)(2,1)S(1)} %assemble_shards.2.rows_in), custom_call_target="tpu_custom_call" | custom-call | tf_op jit(solution)/shard_map/enter_block/pallas_call | solution.py:164
  94.9 1.9 %enter_block.2.hidden = bf16[128,2304]{1,0:T(8,128)(2,1)S(1)} custom-call(bf16[128,1024]{1,0:T(8,128)(2,1)S(1)} %collective-permute-done.1.arrived, f32[7,1024]{1,0:T(8,128)S(1)} %pad_maximum_fusion.1.rows, f32[1,2304]{1,0:T(1,128)S(1)} %broadcast_select_fusion.bias, bf16[2304,1024]{1,0:T(8,128)(2,1)S(1)} %assemble_shards.2.rows_in), custom_call_target="tpu_custom_call" | custom-call | tf_op jit(solution)/shard_map/enter_block/pallas_call | solution.py:164
  98.3 2.5 %section_block.8.refs_0_ = bf16[128,1024]{1,0:T(8,128)(2,1)S(1)} custom-call(bf16[128,1024]{1,0:T(8,128)(2,1)S(1)} %collective-permute-done.23.arrived.refs_1_, bf16[384,1024]{1,0:T(8,128)(2,1)S(1)} %collective-permute-done.24.fresh, f32[7,1024]{1,0:T(8,128)S(1)} %pad_maximum_fusion.1.rows, f32[1,2304]{1,0:T(1,128)S(1)} %broadcast_select_fusion.bias, ...), custom_call_target="tpu_custom_call" | custom-call | tf_op jit(solution)/shard_map/section_block/pallas_call | solution.py:213
  101.6 2.5 %section_block.6.refs_0_ = bf16[128,1024]{1,0:T(8,128)(2,1)S(1)} custom-call(bf16[128,1024]{1,0:T(8,128)(2,1)S(1)} %collective-permute-done.19.arrived.refs_1_, bf16[384,1024]{1,0:T(8,128)(2,1)S(1)} %collective-permute-done.20.fresh, f32[7,1024]{1,0:T(8,128)S(1)} %pad_maximum_fusion.1.rows, f32[1,2304]{1,0:T(1,128)S(1)} %broadcast_select_fusion.bias, ...), custom_call_target="tpu_custom_call" | custom-call | tf_op jit(solution)/shard_map/section_block/pallas_call | solution.py:213
  105.0 2.5 %section_block.9 = (bf16[128,1024]{1,0:T(8,128)(2,1)S(1)}, bf16[256,1024]{1,0:T(8,128)(2,1)S(1)}, bf16[256,1024]{1,0:T(8,128)(2,1)S(1)}) custom-call(bf16[128,1024]{1,0:T(8,128)(2,1)S(1)} %collective-permute-done.25.arrived, bf16[384,1024]{1,0:T(8,128)(2,1)S(1)} %collective-permute-done.24.fresh, f32[7,1024]{1,0:T(8,128)S(1)} %pad_maximum_fusion.1.rows, ...), custom_call_target="tpu_custom_call" | custom-call | tf_op jit(solution)/shard_map/section_block/pallas_call | solution.py:213
  108.2 2.5 %section_block.7 = (bf16[128,1024]{1,0:T(8,128)(2,1)S(1)}, bf16[256,1024]{1,0:T(8,128)(2,1)S(1)}, bf16[256,1024]{1,0:T(8,128)(2,1)S(1)}) custom-call(bf16[128,1024]{1,0:T(8,128)(2,1)S(1)} %collective-permute-done.21.arrived, bf16[384,1024]{1,0:T(8,128)(2,1)S(1)} %collective-permute-done.20.fresh, f32[7,1024]{1,0:T(8,128)S(1)} %pad_maximum_fusion.1.rows, ...), custom_call_target="tpu_custom_call" | custom-call | tf_op jit(solution)/shard_map/section_block/pallas_call | solution.py:213
  112.8 2.5 %section_block.11 = bf16[128,1024]{1,0:T(8,128)(2,1)S(1)} custom-call(bf16[128,1024]{1,0:T(8,128)(2,1)S(1)} %collective-permute-done.31.arrived, bf16[384,1024]{1,0:T(8,128)(2,1)S(1)} %collective-permute-done.24.fresh, f32[7,1024]{1,0:T(8,128)S(1)} %pad_maximum_fusion.1.rows, f32[1,2304]{1,0:T(1,128)S(1)} %broadcast_select_fusion.bias, ...), custom_call_target="tpu_custom_call" | custom-call | tf_op jit(solution)/shard_map/section_block/pallas_call | solution.py:213
  116.0 2.5 %section_block.10 = bf16[128,1024]{1,0:T(8,128)(2,1)S(1)} custom-call(bf16[128,1024]{1,0:T(8,128)(2,1)S(1)} %collective-permute-done.29.arrived, bf16[384,1024]{1,0:T(8,128)(2,1)S(1)} %collective-permute-done.20.fresh, f32[7,1024]{1,0:T(8,128)S(1)} %pad_maximum_fusion.1.rows, f32[1,2304]{1,0:T(1,128)S(1)} %broadcast_select_fusion.bias, ...), custom_call_target="tpu_custom_call" | custom-call | tf_op jit(solution)/shard_map/section_block/pallas_call | solution.py:213
  122.7 33.0 %collective-permute-done.33.refs_8_ = bf16[128,1024]{1,0:T(8,128)(2,1)S(1)} collective-permute-done((bf16[128,1024]{1,0:T(8,128)(2,1)S(1)}, bf16[128,1024]{1,0:T(8,128)(2,1)S(1)}, u32[]{:S(2)}, u32[]{:S(2)}) %collective-permute-start.33) | collective-permute-done | bytes 262176 | tf_op jit(solution)/shard_map/ppermute | solution.py:106
  158.3 16.7 %collective-permute-done.30.refs_6_ = bf16[128,1024]{1,0:T(8,128)(2,1)S(1)} collective-permute-done((bf16[128,1024]{1,0:T(8,128)(2,1)S(1)}, bf16[128,1024]{1,0:T(8,128)(2,1)S(1)}, u32[]{:S(2)}, u32[]{:S(2)}) %collective-permute-start.30) | collective-permute-done | bytes 262176 | tf_op jit(solution)/shard_map/ppermute | solution.py:106
  (94 shorter events, 32.3 us)
Async XLA Ops:
  0.0 52.7 %collective-permute-start.6 = (bf16[576,1024]{1,0:T(8,128)(2,1)}, bf16[576,1024]{1,0:T(8,128)(2,1)}, u32[]{:S(2)}, u32[]{:S(2)}) collective-permute-start(bf16[576,1024]{1,0:T(8,128)(2,1)} %bitcast.17), channel_id=1, source_target_pairs={{2,5},{7,2},{11,14},{14,9},{18,21},{23,18},{27,30},{30,25}} | collective-permute-start | bytes 3538952 | tf_op jit(solution)/shard_map/ppermute | solution.py:106
  1.7 52.7 %collective-permute-start.8 = (bf16[576,1024]{1,0:T(8,128)(2,1)}, bf16[576,1024]{1,0:T(8,128)(2,1)S(1)}, u32[]{:S(2)}, u32[]{:S(2)}) collective-permute-start(bf16[576,1024]{1,0:T(8,128)(2,1)} %bitcast.18), channel_id=1, source_target_pairs={{3,1},{0,5},{4,6},{5,2},{8,10},{9,14},{15,13},{12,9},{19,17},{16,2... | collective-permute-start | bytes 3538952 | tf_op jit(solution)/shard_map/ppermute | solution.py:106
  5.1 50.9 %collective-permute-start.10 = (bf16[576,1024]{1,0:T(8,128)(2,1)}, bf16[576,1024]{1,0:T(8,128)(2,1)S(1)}, u32[]{:S(2)}, u32[]{:S(2)}) collective-permute-start(bf16[576,1024]{1,0:T(8,128)(2,1)} %bitcast.19), channel_id=1, source_target_pairs={{1,5},{6,2},{10,14},{13,9},{17,21},{22,18},{26,30},{29,25}} | collective-permute-start | bytes 3538952 | tf_op jit(solution)/shard_map/ppermute | solution.py:106
  5.9 38.8 %collective-permute-start.17 = (bf16[128,1024]{1,0:T(8,128)(2,1)}, bf16[128,1024]{1,0:T(8,128)(2,1)S(1)}, u32[]{:S(2)}, u32[]{:S(2)}) collective-permute-start(bf16[128,1024]{1,0:T(8,128)(2,1)} %bitcast.26), channel_id=1, source_target_pairs={{1,1},{2,5},{5,2},{6,6},{9,10},{10,14},{13,9},{14,13},{17,17},{18,... | collective-permute-start | bytes 786440 | tf_op jit(solution)/shard_map/ppermute | solution.py:106
  6.6 22.6 %collective-permute-start.2 = (bf16[1,576]{1,0:T(2,128)(2,1)}, bf16[1,576]{1,0:T(2,128)(2,1)S(1)}, u32[]{:S(2)}, u32[]{:S(2)}) collective-permute-start(bf16[1,576]{1,0:T(2,128)(2,1)} %param.12), channel_id=1, source_target_pairs={{1,0},{2,1},{3,2},{0,3},{5,4},{6,5},{7,6},{4,7},{9,8},{10,9},{11,1... | collective-permute-start | bytes 3464 | tf_op jit(solution)/shard_map/ppermute | solution.py:343
  43.0 23.5 %collective-permute-start.11 = (bf16[576,1024]{1,0:T(8,128)(2,1)}, bf16[576,1024]{1,0:T(8,128)(2,1)}, u32[]{:S(2)}, u32[]{:S(2)}) collective-permute-start(bf16[576,1024]{1,0:T(8,128)(2,1)} %bitcast.21), channel_id=1, source_target_pairs={{2,5},{7,2},{11,14},{14,9},{18,21},{23,18},{27,30},{30,25}} | collective-permute-start | bytes 3538952 | tf_op jit(solution)/shard_map/ppermute | solution.py:106
  45.4 31.7 %collective-permute-start.13 = (bf16[576,1024]{1,0:T(8,128)(2,1)}, bf16[576,1024]{1,0:T(8,128)(2,1)S(1)}, u32[]{:S(2)}, u32[]{:S(2)}) collective-permute-start(bf16[576,1024]{1,0:T(8,128)(2,1)} %bitcast.22), channel_id=1, source_target_pairs={{3,1},{0,5},{4,6},{5,2},{8,10},{9,14},{15,13},{12,9},{19,17},{16,2... | collective-permute-start | bytes 3538952 | tf_op jit(solution)/shard_map/ppermute | solution.py:106
  52.7 25.9 %collective-permute-start.15 = (bf16[576,1024]{1,0:T(8,128)(2,1)}, bf16[576,1024]{1,0:T(8,128)(2,1)}, u32[]{:S(2)}, u32[]{:S(2)}) collective-permute-start(bf16[576,1024]{1,0:T(8,128)(2,1)} %bitcast.23), channel_id=1, source_target_pairs={{1,5},{6,2},{10,14},{13,9},{17,21},{22,18},{26,30},{29,25}} | collective-permute-start | bytes 3538952 | tf_op jit(solution)/shard_map/ppermute | solution.py:106
  54.4 24.9 %collective-permute-start.7 = (bf16[576,1024]{1,0:T(8,128)(2,1)}, bf16[576,1024]{1,0:T(8,128)(2,1)}, u32[]{:S(2)}, u32[]{:S(2)}) collective-permute-start(bf16[576,1024]{1,0:T(8,128)(2,1)} %collective-permute-done.6.refs_5_), channel_id=1, source_target_pairs={{5,1},{2,6},{14,10},{9,13},{21,17},{18,22},{30,26},{25,29}} | collective-permute-start | bytes 3538952 | tf_op jit(solution)/shard_map/ppermute | solution.py:106
  57.1 23.0 %collective-permute-start.9 = (bf16[576,1024]{1,0:T(8,128)(2,1)S(1)}, bf16[576,1024]{1,0:T(8,128)(2,1)S(1)}, u32[]{:S(2)}, u32[]{:S(2)}) collective-permute-start(bf16[576,1024]{1,0:T(8,128)(2,1)S(1)} %collective-permute-done.8.refs_2_.refs_7_), channel_id=1, source_target_pairs={{1,5},{5,1},{2,6},{6,2},{10,14},{14,10},{9,13},{13,9},{17,21},{21,... | collective-permute-start | bytes 3538952 | tf_op jit(solution)/shard_map/ppermute | solution.py:106
  66.5 25.7 %collective-permute-start.12 = (bf16[576,1024]{1,0:T(8,128)(2,1)}, bf16[576,1024]{1,0:T(8,128)(2,1)S(1)}, u32[]{:S(2)}, u32[]{:S(2)}) collective-permute-start(bf16[576,1024]{1,0:T(8,128)(2,1)} %collective-permute-done.11.refs_5_), channel_id=1, source_target_pairs={{5,1},{2,6},{14,10},{9,13},{21,17},{18,22},{30,26},{25,29}} | collective-permute-start | bytes 3538952 | tf_op jit(solution)/shard_map/ppermute | solution.py:106
  77.1 15.2 %collective-permute-start.14 = (bf16[576,1024]{1,0:T(8,128)(2,1)S(1)}, bf16[576,1024]{1,0:T(8,128)(2,1)S(1)}, u32[]{:S(2)}, u32[]{:S(2)}) collective-permute-start(bf16[576,1024]{1,0:T(8,128)(2,1)S(1)} %collective-permute-done.13.refs_2_.refs_7_), channel_id=1, source_target_pairs={{1,5},{5,1},{2,6},{6,2},{10,14},{14,10},{9,13},{13,9},{17,21},{21,... | collective-permute-start | bytes 3538952 | tf_op jit(solution)/shard_map/ppermute | solution.py:106
  78.6 19.7 %collective-permute-start.24 = (bf16[384,1024]{1,0:T(8,128)(2,1)S(1)}, bf16[384,1024]{1,0:T(8,128)(2,1)S(1)}, u32[]{:S(2)}, u32[]{:S(2)}) collective-permute-start(bf16[384,1024]{1,0:T(8,128)(2,1)S(1)} %pad_maximum_fusion), channel_id=1, source_target_pairs={{1,1},{2,5}} | collective-permute-start | bytes 2359304 | tf_op jit(solution)/shard_map/ppermute | solution.py:106
  79.4 22.2 %collective-permute-start.20 = (bf16[384,1024]{1,0:T(8,128)(2,1)S(1)}, bf16[384,1024]{1,0:T(8,128)(2,1)S(1)}, u32[]{:S(2)}, u32[]{:S(2)}) collective-permute-start(bf16[384,1024]{1,0:T(8,128)(2,1)S(1)} %pad_maximum_fusion), channel_id=1, source_target_pairs={{0,1},{3,5}} | collective-permute-start | bytes 2359304 | tf_op jit(solution)/shard_map/ppermute | solution.py:106
  80.1 14.8 %collective-permute-start.1 = (bf16[128,1024]{1,0:T(8,128)(2,1)S(1)}, bf16[128,1024]{1,0:T(8,128)(2,1)S(1)}, u32[]{:S(2)}, u32[]{:S(2)}) collective-permute-start(bf16[128,1024]{1,0:T(8,128)(2,1)S(1)} %bitcast.27), channel_id=1, source_target_pairs={{0,1},{3,5},{4,2},{7,6},{8,10},{11,14},{12,9},{15,13},{16,17},{19,... | collective-permute-start | bytes 786440 | tf_op jit(solution)/shard_map/ppermute | solution.py:106
  111.4 9.1 %collective-permute-start.18 = (bf16[128,1024]{1,0:T(8,128)(2,1)S(1)}, bf16[128,1024]{1,0:T(8,128)(2,1)S(1)}, u32[]{:S(2)}, u32[]{:S(2)}) collective-permute-start(bf16[128,1024]{1,0:T(8,128)(2,1)S(1)} %leave_block.3), channel_id=1, source_target_pairs={{25,1},{29,2},{1,5},{2,9},{6,10},{14,14},{9,17},{13,18},{17,21},{1... | collective-permute-start | bytes 786440 | tf_op jit(solution)/shard_map/ppermute | solution.py:106
  112.1 9.2 %collective-permute-start.16 = (bf16[128,1024]{1,0:T(8,128)(2,1)S(1)}, bf16[128,1024]{1,0:T(8,128)(2,1)S(1)}, u32[]{:S(2)}, u32[]{:S(2)}) collective-permute-start(bf16[128,1024]{1,0:T(8,128)(2,1)S(1)} %leave_block.2), channel_id=1, source_target_pairs={{25,0},{29,3},{1,4},{2,8},{6,11},{14,15},{9,16},{13,19},{17,20},{1... | collective-permute-start | bytes 786440 | tf_op jit(solution)/shard_map/ppermute | solution.py:106
  118.5 37.1 %collective-permute-start.33 = (bf16[128,1024]{1,0:T(8,128)(2,1)S(1)}, bf16[128,1024]{1,0:T(8,128)(2,1)S(1)}, u32[]{:S(2)}, u32[]{:S(2)}) collective-permute-start(bf16[128,1024]{1,0:T(8,128)(2,1)S(1)} %section_block.10), channel_id=1, source_target_pairs={{25,0},{29,3},{1,4},{5,7},{2,8},{6,11},{10,12},{14,15},{9,16},{13,... | collective-permute-start | bytes 786440 | tf_op jit(solution)/shard_map/ppermute | solution.py:106
  119.8 38.4 %collective-permute-start.26 = (bf16[256,1024]{1,0:T(8,128)(2,1)S(1)}, bf16[256,1024]{1,0:T(8,128)(2,1)S(1)}, u32[]{:S(2)}, u32[]{:S(2)}) collective-permute-start(bf16[256,1024]{1,0:T(8,128)(2,1)S(1)} %get-tuple-element.12), channel_id=1, source_target_pairs={{25,1},{29,2},{1,5},{2,9},{6,10},{14,14},{9,17},{13,18},{17,21},{1... | collective-permute-start | bytes 1572872 | tf_op jit(solution)/shard_map/ppermute | solution.py:106
  120.5 37.7 %collective-permute-start.28 = (bf16[256,1024]{1,0:T(8,128)(2,1)S(1)}, bf16[256,1024]{1,0:T(8,128)(2,1)S(1)}, u32[]{:S(2)}, u32[]{:S(2)}) collective-permute-start(bf16[256,1024]{1,0:T(8,128)(2,1)S(1)} %get-tuple-element.14), channel_id=1, source_target_pairs={{6,6},{9,13},{22,22},{25,29}} | collective-permute-start | bytes 1572872 | tf_op jit(solution)/shard_map/ppermute | solution.py:106
  121.3 53.7 %collective-permute-start.22 = (bf16[256,1024]{1,0:T(8,128)(2,1)S(1)}, bf16[256,1024]{1,0:T(8,128)(2,1)S(1)}, u32[]{:S(2)}, u32[]{:S(2)}) collective-permute-start(bf16[256,1024]{1,0:T(8,128)(2,1)S(1)} %get-tuple-element.11), channel_id=1, source_target_pairs={{25,0},{29,3},{1,4},{2,8},{6,11},{14,15},{9,16},{13,19},{17,20},{1... | collective-permute-start | bytes 1572872 | tf_op jit(solution)/shard_map/ppermute | solution.py:106
  122.0 35.0 %collective-permute-start.32 = (bf16[128,1024]{1,0:T(8,128)(2,1)S(1)}, bf16[128,1024]{1,0:T(8,128)(2,1)S(1)}, u32[]{:S(2)}, u32[]{:S(2)}) collective-permute-start(bf16[128,1024]{1,0:T(8,128)(2,1)S(1)} %collective-permute-done.31.arrived), channel_id=1, source_target_pairs={{6,6},{9,13},{22,22},{25,29}} | collective-permute-start | bytes 786440 | tf_op jit(solution)/shard_map/ppermute | solution.py:106
  155.6 19.3 %collective-permute-start.27 = (bf16[256,1024]{1,0:T(8,128)(2,1)S(1)}, bf16[256,1024]{1,0:T(8,128)(2,1)S(1)}, u32[]{:S(2)}, u32[]{:S(2)}) collective-permute-start(bf16[256,1024]{1,0:T(8,128)(2,1)S(1)} %get-tuple-element.13), channel_id=1, source_target_pairs={{6,7},{9,12},{22,23},{25,28}} | collective-permute-start | bytes 1572872 | tf_op jit(solution)/shard_map/ppermute | solution.py:106
  156.9 18.0 %collective-permute-start.30 = (bf16[128,1024]{1,0:T(8,128)(2,1)S(1)}, bf16[128,1024]{1,0:T(8,128)(2,1)S(1)}, u32[]{:S(2)}, u32[]{:S(2)}) collective-permute-start(bf16[128,1024]{1,0:T(8,128)(2,1)S(1)} %collective-permute-done.29.arrived), channel_id=1, source_target_pairs={{6,7},{9,12},{22,23},{25,28}} | collective-permute-start | bytes 786440 | tf_op jit(solution)/shard_map/ppermute | solution.py:106
  (23 other events, 201.3 us)

commit v4 on v3

--- a/solution.py
+++ b/solution.py
@@ -70,8 +70,8 @@
 
     def hop_pairs(self):
         return [
-            (self.worker(section, core), self.worker((section + 1) % self.sections, core))
-            for section in range(self.sections)
+            (self.worker(section, core), self.worker(section + 1, core))
+            for section in range(self.sections - 1)
             for core in range(2)
         ]
 
@@ -183,7 +183,7 @@
     )(arrived, hidden, rows, full_out)
 
 
-def block_kernel(first_row, arrived, fresh, rows, bias, rows_in, rows_out, *refs):
+def block_kernel(first_row, box_products, arrived, fresh, rows, bias, rows_in, rows_out, *refs):
     size = arrived.shape[0]
     new = fresh[first_row : first_row + size, :].astype(jnp.float32)
     current = jnp.where(row(rows, FIRST) == 1.0, new, arrived[...].astype(jnp.float32))
@@ -197,21 +197,19 @@
     if len(refs) == 1:
         refs[0][...] = result
         return
-    product, arrival, produced, products, arrivals = refs
+    kept, produced, box = refs
     produced[...] = result
-    products[:size, :] = product[...]
-    products[size:, :] = result
-    arrivals[:size, :] = arrival[...]
-    arrivals[size:, :] = arrived[...]
-
-
-def run_block(first_row, arrived, fresh, operands, kept=()):
+    box[:size, :] = kept[...]
+    box[size:, :] = result if box_products else arrived[...]
+
+
+def run_block(first_row, arrived, fresh, operands, kept=(), box_products=False):
     vector = pl.BlockSpec(memory_space=pltpu.VMEM)
     size, width = arrived.shape
-    chunks = [1, 2, 2] if kept else [1]
+    chunks = [1, 2] if kept else [1]
     shapes = [jax.ShapeDtypeStruct((count * size, width), arrived.dtype) for count in chunks]
     return pl.pallas_call(
-        functools.partial(block_kernel, first_row),
+        functools.partial(block_kernel, first_row, box_products),
         out_shape=shapes,
         in_specs=[vector] * (6 + len(kept)),
         out_specs=[vector] * len(shapes),
@@ -238,8 +236,8 @@
         records[tick] = jnp.where(is_near == 1.0, mine(close, close_start), mine(far, far_start))
 
     either(0, early, 0, near, 0)
-    either(1, late, 0, near, size)
-    either(2, late, size, near_late, 0)
+    either(1, late, 0, near_late, 0)
+    either(2, late, size, near_late, size)
     records[ticks - 1] = mine(final, 0)
 
 
@@ -357,27 +355,29 @@
     def hop(values):
         return [send(values[slot], places.hop_pairs()) for slot in slots]
 
-    def blocks(tick_index, *kept):
+    def blocks(tick_index, kept=(), box_products=False):
         first_row = (tick_index - 1) * chunk
         made = []
         for slot in slots:
-            chunks = [array[slot] for array in kept]
-            made.append(run_block(first_row, currents[slot], waiting[slot], operands, chunks))
-        return list(zip(*made))
+            chunks = [kept[slot]] if kept else []
+            made.append(
+                run_block(first_row, currents[slot], waiting[slot], operands, chunks, box_products)
+            )
+        return [list(values) for values in zip(*made)]
 
     products = [leave(currents[slot], hiddens[slot], rows, full_out) for slot in slots]
     currents = hop(products)
     early = home(products, 1, False)
-    arrivals = currents
+    near = home(currents, 0, True)
     (products,) = blocks(1)
     currents = hop(products)
-    made, boxed_products, boxed_arrivals = blocks(2, products, arrivals)
-    currents = hop(made)
-    late = home(boxed_products, 1, False)
-    near = home(boxed_arrivals, 0, True)
-    near_late = home(currents, 0, True)
-    (products,) = blocks(3)
+    arrivals = currents
+    products, boxed = blocks(2, products, True)
+    currents = hop(products)
+    late = home(boxed, 1, False)
+    products, boxed = blocks(3, arrivals, False)
     final = home(products, 1, None)
+    near_late = home(boxed, 0, True)
     return collect(rows, early, late, near, near_late, final)[None]
 
 

time: 177 us -> 176 us (level)
  the two profiles are of different devices: /device:TPU:3 before, /device:TPU:0 now
where the time goes in v4:
time: 176 us; the launch traced here: 175 us
  waiting for transfers between devices  78.9 us (45%)
  starting transfers between devices  55 us (31%)
  Pallas kernels  24.7 us (14%)
  local copies, waits for them, and re-layouts  8.06 us (5%)
  between operations  6.46 us (4%)
  other arithmetic  2.14 us (1%)
    ppermute x32, waiting for transfers between devices, send(): return lax.ppermute(value, ('section', 'tensor'), pairs)  54.5 us
    ppermute x32, starting transfers between devices, send(): return lax.ppermute(value, ('section', 'tensor'), pairs)  43.8 us
    ppermute x3, waiting for transfers between devices, collapsed(): biases.append(lax.ppermute(in_bias, 'tensor', pairs))  24.4 us
    pallas_call x6, Pallas kernels, run_block(): pl.pallas_call(functools.partial(block_kernel, first_row, box_products),...  15.1 us
    ppermute x3, starting transfers between devices, collapsed(): biases.append(lax.ppermute(in_bias, 'tensor', pairs))  11.3 us
    pallas_call x2, Pallas kernels, enter(): pl.pallas_call(enter_kernel, out_shape=jax.ShapeDtypeStruct((arrived.shap...  3.77 us
  transfers between devices with their start and end apart: 35, of which 7 were waited for; matrix products, arithmetic and copies ran while one was open for 4% of the time, Pallas kernels for 13%

profile of v4, /device:TPU:0, one launch (start us, length us, event | category | flops | bytes accessed | tf_op | source)
XLA Modules:
  0.0 175.3 jit_solution(12744583597731786003)
XLA Ops:
  0.0 1.7 collective-permute-start.6
  1.7 4.0 %collective-permute-start.8 = (bf16[576,1024]{1,0:T(8,128)(2,1)}, bf16[576,1024]{1,0:T(8,128)(2,1)S(1)}, u32[]{:S(2)}, u32[]{:S(2)}) collective-permute-start(bf16[576,1024]{1,0:T(8,128)(2,1)} %bitcast.18), channel_id=1, source_target_pairs={{3,1},{0,5},{4,6},{5,2},{8,10},{9,14},{15,13},{12,9},{19,17},{16,2... | collective-permute-start | bytes 3538952 | tf_op jit(solution)/shard_map/ppermute | solution.py:106
  7.2 3.4 %collective-permute-start.2 = (bf16[1,576]{1,0:T(2,128)(2,1)}, bf16[1,576]{1,0:T(2,128)(2,1)S(1)}, u32[]{:S(2)}, u32[]{:S(2)}) collective-permute-start(bf16[1,576]{1,0:T(2,128)(2,1)} %param.12), channel_id=1, source_target_pairs={{1,0},{2,1},{3,2},{0,3},{5,4},{6,5},{7,6},{4,7},{9,8},{10,9},{11,1... | collective-permute-start | bytes 3464 | tf_op jit(solution)/shard_map/ppermute | solution.py:341
  10.6 20.9 %collective-permute-done.2 = bf16[1,576]{1,0:T(2,128)(2,1)S(1)} collective-permute-done((bf16[1,576]{1,0:T(2,128)(2,1)}, bf16[1,576]{1,0:T(2,128)(2,1)S(1)}, u32[]{:S(2)}, u32[]{:S(2)}) %collective-permute-start.2) | collective-permute-done | bytes 1184 | tf_op jit(solution)/shard_map/ppermute | solution.py:341
  31.5 4.0 %collective-permute-start.3 = (bf16[1,576]{1,0:T(2,128)(2,1)}, bf16[1,576]{1,0:T(2,128)(2,1)S(1)}, u32[]{:S(2)}, u32[]{:S(2)}) collective-permute-start(bf16[1,576]{1,0:T(2,128)(2,1)} %param.12), channel_id=1, source_target_pairs={{2,0},{3,1},{0,2},{1,3},{6,4},{7,5},{4,6},{5,7},{10,8},{11,9},{8,1... | collective-permute-start | bytes 3464 | tf_op jit(solution)/shard_map/ppermute | solution.py:341
  35.5 1.8 %collective-permute-done.3 = bf16[1,576]{1,0:T(2,128)(2,1)S(1)} collective-permute-done((bf16[1,576]{1,0:T(2,128)(2,1)}, bf16[1,576]{1,0:T(2,128)(2,1)S(1)}, u32[]{:S(2)}, u32[]{:S(2)}) %collective-permute-start.3) | collective-permute-done | bytes 1184 | tf_op jit(solution)/shard_map/ppermute | solution.py:341
  37.3 3.9 %collective-permute-start.4 = (bf16[1,576]{1,0:T(2,128)(2,1)}, bf16[1,576]{1,0:T(2,128)(2,1)S(1)}, u32[]{:S(2)}, u32[]{:S(2)}) collective-permute-start(bf16[1,576]{1,0:T(2,128)(2,1)} %param.12), channel_id=1, source_target_pairs={{3,0},{0,1},{1,2},{2,3},{7,4},{4,5},{5,6},{6,7},{11,8},{8,9},{9,10... | collective-permute-start | bytes 3464 | tf_op jit(solution)/shard_map/ppermute | solution.py:341
  41.1 1.7 collective-permute-done.4
  48.8 7.0 %collective-permute-start.13 = (bf16[576,1024]{1,0:T(8,128)(2,1)}, bf16[576,1024]{1,0:T(8,128)(2,1)S(1)}, u32[]{:S(2)}, u32[]{:S(2)}) collective-permute-start(bf16[576,1024]{1,0:T(8,128)(2,1)} %bitcast.22), channel_id=1, source_target_pairs={{3,1},{0,5},{4,6},{5,2},{8,10},{9,14},{15,13},{12,9},{19,17},{16,2... | collective-permute-start | bytes 3538952 | tf_op jit(solution)/shard_map/ppermute | solution.py:106
  55.8 1.7 collective-permute-start.15
  68.1 2.0 %dynamic-slice_bitcast_fusion.2 = (bf16[128,1024]{1,0:T(8,128)(2,1)}, bf16[128,1024]{1,0:T(8,128)(2,1)}, bf16[128,1024]{1,0:T(8,128)(2,1)}) fusion(bf16[8,128,1024]{2,1,0:T(8,128)(2,1)} %param.17, s32[]{:T(128)S(6)} %select_n.34, s32[]{:T(128)S(6)} %select_n.36, s32[]{:T(128)S(6)} %select_n.35), kind=kLoop, calls=%fused_computation.3 | loop fusion | bytes 1572876 | tf_op jit(solution)/shard_map/jit(dynamic_index_in_dim)/squeeze | solution.py:331
  72.2 9.4 %collective-permute-done.13.refs_2_.refs_7_ = bf16[576,1024]{1,0:T(8,128)(2,1)S(1)} collective-permute-done((bf16[576,1024]{1,0:T(8,128)(2,1)}, bf16[576,1024]{1,0:T(8,128)(2,1)S(1)}, u32[]{:S(2)}, u32[]{:S(2)}) %collective-permute-start.13) | collective-permute-done | bytes 1179680 | tf_op jit(solution)/shard_map/ppermute | solution.py:106
  83.9 5.5 %collective-permute-start.20 = (bf16[384,1024]{1,0:T(8,128)(2,1)S(1)}, bf16[384,1024]{1,0:T(8,128)(2,1)S(1)}, u32[]{:S(2)}, u32[]{:S(2)}) collective-permute-start(bf16[384,1024]{1,0:T(8,128)(2,1)S(1)} %pad_maximum_fusion), channel_id=1, source_target_pairs={{0,1},{3,5}} | collective-permute-start | bytes 2359304 | tf_op jit(solution)/shard_map/ppermute | solution.py:106
  93.9 1.9 %enter_block.3.hidden = bf16[128,2304]{1,0:T(8,128)(2,1)S(1)} custom-call(bf16[128,1024]{1,0:T(8,128)(2,1)S(1)} %copy-done.5, f32[7,1024]{1,0:T(8,128)S(1)} %pad_maximum_fusion.1.rows, f32[1,2304]{1,0:T(1,128)S(1)} %broadcast_select_fusion.bias, bf16[2304,1024]{1,0:T(8,128)(2,1)S(1)} %assemble_shards.2.rows_in), custom_call_target="tpu_custom_call" | custom-call | tf_op jit(solution)/shard_map/enter_block/pallas_call | solution.py:164
  98.5 6.0 %collective-permute-done.1.arrived = bf16[128,1024]{1,0:T(8,128)(2,1)S(1)} collective-permute-done((bf16[128,1024]{1,0:T(8,128)(2,1)S(1)}, bf16[128,1024]{1,0:T(8,128)(2,1)S(1)}, u32[]{:S(2)}, u32[]{:S(2)}) %collective-permute-start.1) | collective-permute-done | bytes 262176 | tf_op jit(solution)/shard_map/ppermute | solution.py:106
  104.5 1.9 %enter_block.2.hidden = bf16[128,2304]{1,0:T(8,128)(2,1)S(1)} custom-call(bf16[128,1024]{1,0:T(8,128)(2,1)S(1)} %collective-permute-done.1.arrived, f32[7,1024]{1,0:T(8,128)S(1)} %pad_maximum_fusion.1.rows, f32[1,2304]{1,0:T(1,128)S(1)} %broadcast_select_fusion.bias, bf16[2304,1024]{1,0:T(8,128)(2,1)S(1)} %assemble_shards.2.rows_in), custom_call_target="tpu_custom_call" | custom-call | tf_op jit(solution)/shard_map/enter_block/pallas_call | solution.py:164
  107.9 2.5 %section_block.8.refs_0_ = bf16[128,1024]{1,0:T(8,128)(2,1)S(1)} custom-call(bf16[128,1024]{1,0:T(8,128)(2,1)S(1)} %collective-permute-done.23.arrived, bf16[384,1024]{1,0:T(8,128)(2,1)S(1)} %collective-permute-done.24.fresh, f32[7,1024]{1,0:T(8,128)S(1)} %pad_maximum_fusion.1.rows, f32[1,2304]{1,0:T(1,128)S(1)} %broadcast_select_fusion.bias, ...), custom_call_target="tpu_custom_call" | custom-call | tf_op jit(solution)/shard_map/section_block/pallas_call | solution.py:211
  111.2 2.5 %section_block.6.refs_0_ = bf16[128,1024]{1,0:T(8,128)(2,1)S(1)} custom-call(bf16[128,1024]{1,0:T(8,128)(2,1)S(1)} %collective-permute-done.19.arrived, bf16[384,1024]{1,0:T(8,128)(2,1)S(1)} %collective-permute-done.20.fresh, f32[7,1024]{1,0:T(8,128)S(1)} %pad_maximum_fusion.1.rows, f32[1,2304]{1,0:T(1,128)S(1)} %broadcast_select_fusion.bias, ...), custom_call_target="tpu_custom_call" | custom-call | tf_op jit(solution)/shard_map/section_block/pallas_call | solution.py:211
  114.6 2.5 %section_block.9 = (bf16[128,1024]{1,0:T(8,128)(2,1)S(1)}, bf16[256,1024]{1,0:T(8,128)(2,1)S(1)}) custom-call(bf16[128,1024]{1,0:T(8,128)(2,1)S(1)} %collective-permute-done.25.arrived.refs_0_, bf16[384,1024]{1,0:T(8,128)(2,1)S(1)} %collective-permute-done.24.fresh, f32[7,1024]{1,0:T(8,128)S(1)} %pad_maximum_fusion.1.rows, ...), custom_call_target="tpu_custom_call" | custom-call | tf_op jit(solution)/shard_map/section_block/pallas_call | solution.py:211
  117.8 2.5 %section_block.7 = (bf16[128,1024]{1,0:T(8,128)(2,1)S(1)}, bf16[256,1024]{1,0:T(8,128)(2,1)S(1)}) custom-call(bf16[128,1024]{1,0:T(8,128)(2,1)S(1)} %collective-permute-done.21.arrived.refs_0_, bf16[384,1024]{1,0:T(8,128)(2,1)S(1)} %collective-permute-done.20.fresh, f32[7,1024]{1,0:T(8,128)S(1)} %pad_maximum_fusion.1.rows, ...), custom_call_target="tpu_custom_call" | custom-call | tf_op jit(solution)/shard_map/section_block/pallas_call | solution.py:211
  124.4 2.5 %section_block.11 = (bf16[128,1024]{1,0:T(8,128)(2,1)S(1)}, bf16[256,1024]{1,0:T(8,128)(2,1)S(1)}) custom-call(bf16[128,1024]{1,0:T(8,128)(2,1)S(1)} %collective-permute-done.31.arrived, bf16[384,1024]{1,0:T(8,128)(2,1)S(1)} %collective-permute-done.24.fresh, f32[7,1024]{1,0:T(8,128)S(1)} %pad_maximum_fusion.1.rows, ...), custom_call_target="tpu_custom_call" | custom-call | tf_op jit(solution)/shard_map/section_block/pallas_call | solution.py:211
  127.6 2.5 %section_block.10 = (bf16[128,1024]{1,0:T(8,128)(2,1)S(1)}, bf16[256,1024]{1,0:T(8,128)(2,1)S(1)}) custom-call(bf16[128,1024]{1,0:T(8,128)(2,1)S(1)} %collective-permute-done.29.arrived, bf16[384,1024]{1,0:T(8,128)(2,1)S(1)} %collective-permute-done.20.fresh, f32[7,1024]{1,0:T(8,128)S(1)} %pad_maximum_fusion.1.rows, ...), custom_call_target="tpu_custom_call" | custom-call | tf_op jit(solution)/shard_map/section_block/pallas_call | solution.py:211
  131.4 15.3 %collective-permute-done.16.refs_0_ = bf16[128,1024]{1,0:T(8,128)(2,1)S(1)} collective-permute-done((bf16[128,1024]{1,0:T(8,128)(2,1)S(1)}, bf16[128,1024]{1,0:T(8,128)(2,1)S(1)}, u32[]{:S(2)}, u32[]{:S(2)}) %collective-permute-start.16) | collective-permute-done | bytes 262176 | tf_op jit(solution)/shard_map/ppermute | solution.py:106
  150.2 23.7 %collective-permute-done.33.refs_8_ = bf16[128,1024]{1,0:T(8,128)(2,1)S(1)} collective-permute-done((bf16[128,1024]{1,0:T(8,128)(2,1)S(1)}, bf16[128,1024]{1,0:T(8,128)(2,1)S(1)}, u32[]{:S(2)}, u32[]{:S(2)}) %collective-permute-start.33) | collective-permute-done | bytes 262176 | tf_op jit(solution)/shard_map/ppermute | solution.py:106
  (94 shorter events, 37.8 us)
Async XLA Ops:
  0.0 55.8 %collective-permute-start.6 = (bf16[576,1024]{1,0:T(8,128)(2,1)}, bf16[576,1024]{1,0:T(8,128)(2,1)}, u32[]{:S(2)}, u32[]{:S(2)}) collective-permute-start(bf16[576,1024]{1,0:T(8,128)(2,1)} %bitcast.17), channel_id=1, source_target_pairs={{2,5},{7,2},{11,14},{14,9},{18,21},{23,18},{27,30},{30,25}} | collective-permute-start | bytes 3538952 | tf_op jit(solution)/shard_map/ppermute | solution.py:106
  1.7 55.7 %collective-permute-start.8 = (bf16[576,1024]{1,0:T(8,128)(2,1)}, bf16[576,1024]{1,0:T(8,128)(2,1)S(1)}, u32[]{:S(2)}, u32[]{:S(2)}) collective-permute-start(bf16[576,1024]{1,0:T(8,128)(2,1)} %bitcast.18), channel_id=1, source_target_pairs={{3,1},{0,5},{4,6},{5,2},{8,10},{9,14},{15,13},{12,9},{19,17},{16,2... | collective-permute-start | bytes 3538952 | tf_op jit(solution)/shard_map/ppermute | solution.py:106
  5.8 60.6 %collective-permute-start.10 = (bf16[576,1024]{1,0:T(8,128)(2,1)}, bf16[576,1024]{1,0:T(8,128)(2,1)S(1)}, u32[]{:S(2)}, u32[]{:S(2)}) collective-permute-start(bf16[576,1024]{1,0:T(8,128)(2,1)} %bitcast.19), channel_id=1, source_target_pairs={{1,5},{6,2},{10,14},{13,9},{17,21},{22,18},{26,30},{29,25}} | collective-permute-start | bytes 3538952 | tf_op jit(solution)/shard_map/ppermute | solution.py:106
  6.5 41.5 %collective-permute-start.17 = (bf16[128,1024]{1,0:T(8,128)(2,1)}, bf16[128,1024]{1,0:T(8,128)(2,1)S(1)}, u32[]{:S(2)}, u32[]{:S(2)}) collective-permute-start(bf16[128,1024]{1,0:T(8,128)(2,1)} %bitcast.26), channel_id=1, source_target_pairs={{1,1},{2,5},{5,2},{6,6},{9,10},{10,14},{13,9},{14,13},{17,17},{18,... | collective-permute-start | bytes 786440 | tf_op jit(solution)/shard_map/ppermute | solution.py:106
  7.2 24.3 %collective-permute-start.2 = (bf16[1,576]{1,0:T(2,128)(2,1)}, bf16[1,576]{1,0:T(2,128)(2,1)S(1)}, u32[]{:S(2)}, u32[]{:S(2)}) collective-permute-start(bf16[1,576]{1,0:T(2,128)(2,1)} %param.12), channel_id=1, source_target_pairs={{1,0},{2,1},{3,2},{0,3},{5,4},{6,5},{7,6},{4,7},{9,8},{10,9},{11,1... | collective-permute-start | bytes 3464 | tf_op jit(solution)/shard_map/ppermute | solution.py:341
  46.4 25.1 %collective-permute-start.11 = (bf16[576,1024]{1,0:T(8,128)(2,1)}, bf16[576,1024]{1,0:T(8,128)(2,1)}, u32[]{:S(2)}, u32[]{:S(2)}) collective-permute-start(bf16[576,1024]{1,0:T(8,128)(2,1)} %bitcast.21), channel_id=1, source_target_pairs={{2,5},{7,2},{11,14},{14,9},{18,21},{23,18},{27,30},{30,25}} | collective-permute-start | bytes 3538952 | tf_op jit(solution)/shard_map/ppermute | solution.py:106
  48.8 32.8 %collective-permute-start.13 = (bf16[576,1024]{1,0:T(8,128)(2,1)}, bf16[576,1024]{1,0:T(8,128)(2,1)S(1)}, u32[]{:S(2)}, u32[]{:S(2)}) collective-permute-start(bf16[576,1024]{1,0:T(8,128)(2,1)} %bitcast.22), channel_id=1, source_target_pairs={{3,1},{0,5},{4,6},{5,2},{8,10},{9,14},{15,13},{12,9},{19,17},{16,2... | collective-permute-start | bytes 3538952 | tf_op jit(solution)/shard_map/ppermute | solution.py:106
  55.8 27.4 %collective-permute-start.15 = (bf16[576,1024]{1,0:T(8,128)(2,1)}, bf16[576,1024]{1,0:T(8,128)(2,1)}, u32[]{:S(2)}, u32[]{:S(2)}) collective-permute-start(bf16[576,1024]{1,0:T(8,128)(2,1)} %bitcast.23), channel_id=1, source_target_pairs={{1,5},{6,2},{10,14},{13,9},{17,21},{22,18},{26,30},{29,25}} | collective-permute-start | bytes 3538952 | tf_op jit(solution)/shard_map/ppermute | solution.py:106
  57.5 26.4 %collective-permute-start.7 = (bf16[576,1024]{1,0:T(8,128)(2,1)}, bf16[576,1024]{1,0:T(8,128)(2,1)}, u32[]{:S(2)}, u32[]{:S(2)}) collective-permute-start(bf16[576,1024]{1,0:T(8,128)(2,1)} %collective-permute-done.6.refs_5_), channel_id=1, source_target_pairs={{5,1},{2,6},{14,10},{9,13},{21,17},{18,22},{30,26},{25,29}} | collective-permute-start | bytes 3538952 | tf_op jit(solution)/shard_map/ppermute | solution.py:106
  67.4 22.1 %collective-permute-start.9 = (bf16[576,1024]{1,0:T(8,128)(2,1)S(1)}, bf16[576,1024]{1,0:T(8,128)(2,1)S(1)}, u32[]{:S(2)}, u32[]{:S(2)}) collective-permute-start(bf16[576,1024]{1,0:T(8,128)(2,1)S(1)} %collective-permute-done.8.refs_2_.refs_7_), channel_id=1, source_target_pairs={{1,5},{5,1},{2,6},{6,2},{10,14},{14,10},{9,13},{13,9},{17,21},{21,... | collective-permute-start | bytes 3538952 | tf_op jit(solution)/shard_map/ppermute | solution.py:106
  71.5 24.3 %collective-permute-start.12 = (bf16[576,1024]{1,0:T(8,128)(2,1)}, bf16[576,1024]{1,0:T(8,128)(2,1)S(1)}, u32[]{:S(2)}, u32[]{:S(2)}) collective-permute-start(bf16[576,1024]{1,0:T(8,128)(2,1)} %collective-permute-done.11.refs_5_), channel_id=1, source_target_pairs={{5,1},{2,6},{14,10},{9,13},{21,17},{18,22},{30,26},{25,29}} | collective-permute-start | bytes 3538952 | tf_op jit(solution)/shard_map/ppermute | solution.py:106
  81.6 14.2 %collective-permute-start.14 = (bf16[576,1024]{1,0:T(8,128)(2,1)S(1)}, bf16[576,1024]{1,0:T(8,128)(2,1)S(1)}, u32[]{:S(2)}, u32[]{:S(2)}) collective-permute-start(bf16[576,1024]{1,0:T(8,128)(2,1)S(1)} %collective-permute-done.13.refs_2_.refs_7_), channel_id=1, source_target_pairs={{1,5},{5,1},{2,6},{6,2},{10,14},{14,10},{9,13},{13,9},{17,21},{21,... | collective-permute-start | bytes 3538952 | tf_op jit(solution)/shard_map/ppermute | solution.py:106
  83.1 24.8 %collective-permute-start.24 = (bf16[384,1024]{1,0:T(8,128)(2,1)S(1)}, bf16[384,1024]{1,0:T(8,128)(2,1)S(1)}, u32[]{:S(2)}, u32[]{:S(2)}) collective-permute-start(bf16[384,1024]{1,0:T(8,128)(2,1)S(1)} %pad_maximum_fusion), channel_id=1, source_target_pairs={{1,1},{2,5}} | collective-permute-start | bytes 2359304 | tf_op jit(solution)/shard_map/ppermute | solution.py:106
  83.9 27.2 %collective-permute-start.20 = (bf16[384,1024]{1,0:T(8,128)(2,1)S(1)}, bf16[384,1024]{1,0:T(8,128)(2,1)S(1)}, u32[]{:S(2)}, u32[]{:S(2)}) collective-permute-start(bf16[384,1024]{1,0:T(8,128)(2,1)S(1)} %pad_maximum_fusion), channel_id=1, source_target_pairs={{0,1},{3,5}} | collective-permute-start | bytes 2359304 | tf_op jit(solution)/shard_map/ppermute | solution.py:106
  89.5 15.0 %collective-permute-start.1 = (bf16[128,1024]{1,0:T(8,128)(2,1)S(1)}, bf16[128,1024]{1,0:T(8,128)(2,1)S(1)}, u32[]{:S(2)}, u32[]{:S(2)}) collective-permute-start(bf16[128,1024]{1,0:T(8,128)(2,1)S(1)} %bitcast.27), channel_id=1, source_target_pairs={{0,1},{3,5},{4,2},{7,6},{8,10},{11,14},{12,9},{15,13},{16,17},{19,... | collective-permute-start | bytes 786440 | tf_op jit(solution)/shard_map/ppermute | solution.py:106
  97.8 10.1 %collective-permute-start.23 = (bf16[128,1024]{1,0:T(8,128)(2,1)S(1)}, bf16[128,1024]{1,0:T(8,128)(2,1)S(1)}, u32[]{:S(2)}, u32[]{:S(2)}) collective-permute-start(bf16[128,1024]{1,0:T(8,128)(2,1)S(1)} %leave_block.3), channel_id=1, source_target_pairs={{1,2},{5,6},{2,10},{6,14},{10,9},{14,13},{9,17},{13,21},{17,18},{2... | collective-permute-start | bytes 786440 | tf_op jit(solution)/shard_map/ppermute | solution.py:106
  121.7 25.1 %collective-permute-start.16 = (bf16[128,1024]{1,0:T(8,128)(2,1)S(1)}, bf16[128,1024]{1,0:T(8,128)(2,1)S(1)}, u32[]{:S(2)}, u32[]{:S(2)}) collective-permute-start(bf16[128,1024]{1,0:T(8,128)(2,1)S(1)} %leave_block.2), channel_id=1, source_target_pairs={{25,0},{29,3},{1,4},{2,8},{6,11},{14,15},{9,16},{13,19},{17,20},{1... | collective-permute-start | bytes 786440 | tf_op jit(solution)/shard_map/ppermute | solution.py:106
  123.0 24.5 %collective-permute-start.28 = (bf16[128,1024]{1,0:T(8,128)(2,1)S(1)}, bf16[128,1024]{1,0:T(8,128)(2,1)S(1)}, u32[]{:S(2)}, u32[]{:S(2)}) collective-permute-start(bf16[128,1024]{1,0:T(8,128)(2,1)S(1)} %collective-permute-done.23.arrived), channel_id=1, source_target_pairs={{6,6},{9,13},{22,22},{25,29}} | collective-permute-start | bytes 786440 | tf_op jit(solution)/shard_map/ppermute | solution.py:106
  123.7 24.5 %collective-permute-start.27 = (bf16[128,1024]{1,0:T(8,128)(2,1)S(1)}, bf16[128,1024]{1,0:T(8,128)(2,1)S(1)}, u32[]{:S(2)}, u32[]{:S(2)}) collective-permute-start(bf16[128,1024]{1,0:T(8,128)(2,1)S(1)} %collective-permute-done.19.arrived), channel_id=1, source_target_pairs={{6,7},{9,12},{22,23},{25,28}} | collective-permute-start | bytes 786440 | tf_op jit(solution)/shard_map/ppermute | solution.py:106
  126.9 47.0 %collective-permute-start.26 = (bf16[256,1024]{1,0:T(8,128)(2,1)S(1)}, bf16[256,1024]{1,0:T(8,128)(2,1)S(1)}, u32[]{:S(2)}, u32[]{:S(2)}) collective-permute-start(bf16[256,1024]{1,0:T(8,128)(2,1)S(1)} %get-tuple-element.14), channel_id=1, source_target_pairs={{25,1},{29,2},{1,5},{2,9},{6,10},{14,14},{9,17},{13,18},{17,21},{1... | collective-permute-start | bytes 1572872 | tf_op jit(solution)/shard_map/ppermute | solution.py:106
  130.1 43.7 %collective-permute-start.22 = (bf16[256,1024]{1,0:T(8,128)(2,1)S(1)}, bf16[256,1024]{1,0:T(8,128)(2,1)S(1)}, u32[]{:S(2)}, u32[]{:S(2)}) collective-permute-start(bf16[256,1024]{1,0:T(8,128)(2,1)S(1)} %get-tuple-element.13), channel_id=1, source_target_pairs={{25,0},{29,3},{1,4},{2,8},{6,11},{14,15},{9,16},{13,19},{17,20},{1... | collective-permute-start | bytes 1572872 | tf_op jit(solution)/shard_map/ppermute | solution.py:106
  147.4 26.4 %collective-permute-start.32 = (bf16[256,1024]{1,0:T(8,128)(2,1)S(1)}, bf16[256,1024]{1,0:T(8,128)(2,1)S(1)}, u32[]{:S(2)}, u32[]{:S(2)}) collective-permute-start(bf16[256,1024]{1,0:T(8,128)(2,1)S(1)} %get-tuple-element.18), channel_id=1, source_target_pairs={{6,6},{9,13},{22,22},{25,29}} | collective-permute-start | bytes 1572872 | tf_op jit(solution)/shard_map/ppermute | solution.py:106
  148.2 25.7 %collective-permute-start.30 = (bf16[256,1024]{1,0:T(8,128)(2,1)S(1)}, bf16[256,1024]{1,0:T(8,128)(2,1)S(1)}, u32[]{:S(2)}, u32[]{:S(2)}) collective-permute-start(bf16[256,1024]{1,0:T(8,128)(2,1)S(1)} %get-tuple-element.16), channel_id=1, source_target_pairs={{6,7},{9,12},{22,23},{25,28}} | collective-permute-start | bytes 1572872 | tf_op jit(solution)/shard_map/ppermute | solution.py:106
  148.9 25.0 %collective-permute-start.33 = (bf16[128,1024]{1,0:T(8,128)(2,1)S(1)}, bf16[128,1024]{1,0:T(8,128)(2,1)S(1)}, u32[]{:S(2)}, u32[]{:S(2)}) collective-permute-start(bf16[128,1024]{1,0:T(8,128)(2,1)S(1)} %get-tuple-element.19), channel_id=1, source_target_pairs={{25,0},{29,3},{1,4},{5,7},{2,8},{6,11},{10,12},{14,15},{9,16},{13,... | collective-permute-start | bytes 786440 | tf_op jit(solution)/shard_map/ppermute | solution.py:106
  (23 other events, 176.3 us)
